TPU v7x, 32 devices: a whole 2x2x4 slice. The times are simulated.
32 devices in a mesh: row: 8 (over y, x, core), col: 4 (over z).
Axes of the slice: x: 2, y: 2, z: 4, core: 2. Of those that a mesh axis runs over, the one named last changes fastest.
Arguments:
- record: float32 [2, 32768], P(None, ('row', 'col')), may hold values from -5 to 5
Outputs:
- spectrum: float32 [256, 256, 2, 2, 256], P('row', 'col')
All inputs are finite; a program needn't handle non-finite values.
Results may differ from a plain program's by a relative error of at most 0.00011.
Values sent between devices are 32-bit elements; how exact they have to be, the bound alone decides.
No kernel may reach another device: no remote copies, remote signals or barrier semaphores. Data moves between devices by JAX's collectives and lax.ppermute only.
A program may use at most 64 MiB of HBM per device.

v0:
```python
import math

import jax
import jax.numpy as jnp
from jax import lax
from jax.sharding import PartitionSpec as P

C = 256
P_SIZE = 256
HOP = 64


highest = lax.Precision.HIGHEST


def passed_along(block, axis, distance):
    devices = range(lax.axis_size(axis))
    route = [(i - distance, i) for i in devices if i - distance in devices]
    return lax.ppermute(block, axis, route)


def spectral_table(length, start_column, width, weights):
    position = jnp.arange(length, dtype=jnp.int32)
    column = start_column + jnp.arange(width, dtype=jnp.int32)
    turns = position[:, None] * column[None, :] % length
    phase = turns.astype(jnp.float32) * (2.0 * math.pi / length)
    cosine = weights[:, None] * jnp.cos(phase)
    sinus = weights[:, None] * jnp.sin(phase)
    upper = jnp.stack([cosine, -sinus], axis=1)
    bottom = jnp.stack([sinus, cosine], axis=1)
    return jnp.stack([upper, bottom], axis=0)


def hann_weights():
    position = jnp.arange(C, dtype=jnp.int32).astype(jnp.float32)
    return (0.5 - 0.5 * jnp.cos(position * (2.0 * math.pi / C))) / math.sqrt(3.0 * C / 8.0)


def framed(samples, amount):
    blocks = samples.reshape(2, amount + C // HOP - 1, HOP)
    return jnp.concatenate(
        [blocks[:, offset : offset + amount] for offset in range(C // HOP)], axis=2
    )


def downconvert(spectra, start_channel, start_frame):
    channel = start_channel + jnp.arange(spectra.shape[1], dtype=jnp.int32)
    moment = start_frame + jnp.arange(spectra.shape[2], dtype=jnp.int32)
    turns = (channel * HOP % C)[:, None] * (moment % C)[None, :] % C
    phase = turns.astype(jnp.float32) * (2.0 * math.pi / C)
    cosine = jnp.cos(phase)
    sinus = jnp.sin(phase)
    real_part = spectra[0] * cosine + spectra[1] * sinus
    imag_part = spectra[1] * cosine - spectra[0] * sinus
    return jnp.stack([real_part, imag_part])


def channelize(frames, start_channel, width, start_frame):
    weights = spectral_table(C, start_channel, width, hann_weights())
    spectra = lax.dot_general(
        weights,
        frames,
        (((0, 1), (0, 2)), ((), ())),
        precision=highest,
        preferred_element_type=jnp.float32,
    )
    return downconvert(spectra, start_channel, start_frame)


def correlate(leading, trailing):
    lead_count = leading.shape[1]
    trail_count = trailing.shape[1]
    windows = leading.shape[2] // P_SIZE
    lead = leading.reshape(2, lead_count, windows, P_SIZE)
    trail = trailing.reshape(2, trail_count, windows, P_SIZE)
    real_part = lead[0][:, None] * trail[0][None] + lead[1][:, None] * trail[1][None]
    imag_part = lead[1][:, None] * trail[0][None] - lead[0][:, None] * trail[1][None]
    weights = spectral_table(
        P_SIZE, 0, P_SIZE, jnp.full((P_SIZE,), 1.0 / math.sqrt(P_SIZE), jnp.float32)
    )
    real_table = weights[0].reshape(P_SIZE, 2 * P_SIZE)
    imag_table = weights[1].reshape(P_SIZE, 2 * P_SIZE)
    dims = (((3,), (0,)), ((), ()))
    result = lax.dot_general(
        real_part, real_table, dims, precision=highest, preferred_element_type=jnp.float32
    )
    result = result + lax.dot_general(
        imag_part, imag_table, dims, precision=highest, preferred_element_type=jnp.float32
    )
    return result.reshape(lead_count, trail_count, windows, 2, P_SIZE)


def local(record):
    row_count = lax.axis_size("row")
    col_count = lax.axis_size("col")
    lead_width = C // row_count
    trail_width = C // col_count
    own_frames = record.shape[1] // HOP
    device = lax.axis_index("row") * col_count + lax.axis_index("col")
    follow = passed_along(record[:, : C - HOP], ("row", "col"), -1)
    frames = framed(jnp.concatenate([record, follow], axis=1), own_frames)
    spectra = channelize(frames, 0, C, device * own_frames)
    shaped = spectra.reshape(2, C, 1, 1, own_frames)
    leading = lax.all_to_all(shaped, "row", split_axis=1, concat_axis=2, tiled=True)
    leading = lax.all_gather(leading, "col", axis=3, tiled=True)
    trailing = lax.all_to_all(shaped, "col", split_axis=1, concat_axis=3, tiled=True)
    trailing = lax.all_gather(trailing, "row", axis=2, tiled=True)
    leading = leading.reshape(2, lead_width, -1)
    trailing = trailing.reshape(2, trail_width, -1)
    return correlate(leading, trailing)


def solution(mesh):
    return jax.shard_map(
        local,
        mesh=mesh,
        in_specs=(P(None, ("row", "col")),),
        out_specs=P("row", "col", None, None, None),
        check_vma=False,
    )
```

profile of v0, /device:TPU:0, one launch (start us, length us, event | category | flops | bytes accessed | tf_op | source)
XLA Modules:
  0.0 90.0 jit_solution(8008926294532363169)
XLA Ops:
  0.0 0.7 slice.43
  0.7 1.3 %collective-permute-start = (f32[2,192]{1,0:T(2,128)S(1)}, f32[2,192]{1,0:T(2,128)S(1)}, u32[]{:S(2)}, u32[]{:S(2)}) collective-permute-start(f32[2,192]{1,0:T(2,128)S(1)} %slice.43), channel_id=1, source_target_pairs={{1,0},{2,1},{3,2},{4,3},{5,4},{6,5},{7,6},{8,7},{9,8},{10,9},{11,1... | collective-permute-start | bytes 4616 | tf_op jit(solution)/shard_map/ppermute | solution.py:19
  2.0 1.0 %fusion.32 = f32[256,1,256]{2,0,1:T(8,128)S(1)} fusion(), kind=kLoop, calls=%fused_computation.40 | loop fusion | flops 1048576 | bytes 262144 | tf_op jit(solution)/shard_map/neg | solution.py:29
  3.0 1.1 %broadcast_multiply_fusion = (f32[256,1,256]{2,0,1:T(8,128)S(1)}, f32[256,1,256]{2,0,1:T(8,128)S(1)}) fusion(), kind=kLoop, calls=%fused_computation.34 | loop fusion | flops 1048576 | bytes 524288 | tf_op jit(solution)/shard_map/mul;broadcast_in_dim;broadcast_in_dim | solution.py:28
  4.1 1.1 %fusion.33 = (f32[256,1,256]{2,0,1:T(8,128)S(1)}, f32[256,1,256]{2,0,1:T(8,128)S(1)}, f32[256,1,256]{2,0,1:T(8,128)S(1)}) fusion(f32[256]{0:T(256)S(1)} %subtract_multiply_fusion), kind=kLoop, calls=%fused_computation.41 | loop fusion | flops 1114112 | bytes 787456 | tf_op jit(solution)/shard_map/neg | solution.py:29
  5.2 0.1 maximum_bitcast_fusion
  5.3 1.9 %collective-permute-done = f32[2,192]{1,0:T(2,128)S(1)} collective-permute-done((f32[2,192]{1,0:T(2,128)S(1)}, f32[2,192]{1,0:T(2,128)S(1)}, u32[]{:S(2)}, u32[]{:S(2)}) %collective-permute-start) | collective-permute-done | bytes 1568 | tf_op jit(solution)/shard_map/ppermute | solution.py:19
  7.2 0.7 pad_maximum_fusion.2
  7.9 0.1 reshape.348
  8.0 0.7 convolution_bitcast_fusion
  8.7 0.2 multiply_add_fusion
  8.8 0.1 copy.17
  9.0 0.9 %reshape.367 = f32[8,1,1024]{2,1,0:T(1,128)} reshape(f32[256,1,1,2,16]{4,3,2,1,0:T(2,128)S(1)} %bitcast.38) | data formatting | bytes 65536
  9.9 7.2 %all-to-all-start = ((f32[8,1,1024]{2,1,0:T(1,128)}), f32[8,1,1024]{2,1,0:T(1,128)S(1)}, u32[]{:S(2)}, u32[]{:S(2)}) async-start(f32[8,1,1024]{2,1,0:T(1,128)} %reshape.367), calls=%async_computation | async-start | bytes 65536 | tf_op jit(solution)/shard_map/all_to_all | solution.py:104
  17.2 0.1 pad_maximum_fusion
  17.2 0.2 copy.25
  17.4 0.2 copy.27
  17.7 0.9 %reshape.365 = f32[4,1,2048]{2,1,0:T(1,128)} reshape(f32[256,1,1,2,16]{4,3,2,1,0:T(2,128)S(1)} %bitcast.39) | data formatting | bytes 65536
  18.6 3.4 %all-to-all-done = f32[8,1,1024]{2,1,0:T(1,128)S(1)} async-done(((f32[8,1,1024]{2,1,0:T(1,128)}), f32[8,1,1024]{2,1,0:T(1,128)S(1)}, u32[]{:S(2)}, u32[]{:S(2)}) %all-to-all-start) | async-done | bytes 32800 | tf_op jit(solution)/shard_map/all_to_all | solution.py:104
  22.0 3.3 %all-to-all-start.1 = ((f32[4,1,2048]{2,1,0:T(1,128)}), f32[4,1,2048]{2,1,0:T(1,128)S(1)}, u32[]{:S(2)}, u32[]{:S(2)}) async-start(f32[4,1,2048]{2,1,0:T(1,128)} %reshape.365), calls=%async_computation.1 | async-start | bytes 65536 | tf_op jit(solution)/shard_map/all_to_all | solution.py:106
  25.3 0.5 broadcast.533
  25.8 0.6 reduce.1
  26.4 0.4 reshape.368
  26.8 0.1 copy.18
  27.0 15.8 %all-gather = f32[2,32,8,4,1,16]{1,5,3,2,4,0:T(8,128)S(1)} all-gather(f32[2,32,8,1,1,16]{1,5,3,2,4,0:T(8,128)S(1)} %bitcast.48), channel_id=2, replica_groups=mesh['row'=8,'col'=4] {'col'}, dimensions={3}, use_global_device_ids=true | all-gather | bytes 163840 | tf_op jit(solution)/shard_map/all_gather | solution.py:105
  42.8 0.1 copy.19
  42.9 0.1 copy.23
  43.0 0.0 all-to-all-done.1
  43.0 0.6 reduce
  43.7 0.4 reshape.366
  44.1 0.1 copy.21
  44.2 9.2 %all-gather.1 = f32[2,64,8,4,1,16]{1,5,3,2,4,0:T(8,128)S(1)} all-gather(f32[2,64,1,4,1,16]{1,5,3,2,4,0:T(8,128)S(1)} %bitcast.49), channel_id=3, replica_groups=mesh['row'=8,'col'=4] {'row'}, dimensions={2}, use_global_device_ids=true | all-gather | bytes 294912 | tf_op jit(solution)/shard_map/all_gather | solution.py:107
  53.5 0.1 copy.22
  53.6 0.1 copy.24
  53.7 7.9 %fusion = f32[32,64,2,512]{3,1,2,0:T(8,128)S(1)} fusion(f32[256,512,1,1]{0,1,3,2:T(8,128)S(1)} %bitcast.41, f32[64,2,256]{2,0,1:T(8,128)S(1)} %copy.24, f32[32,2,256]{2,1,0:T(2,128)S(1)} %copy.23, f32[64,2,256]{2,0,1:T(8,128)S(1)} %copy.22, f32[32,2,256]{2,1,0:T(2,128)S(1)} %copy.19), kind=kOutput, calls=%fused_computation | convolution fusion | flops 6445596672 | bytes 9306112 | tf_op jit(solution)/shard_map/dot_general | solution.py:87
  61.6 9.8 %fusion.8 = f32[32,64,2,512]{3,1,2,0:T(8,128)} fusion(f32[32,64,2,512]{3,1,2,0:T(8,128)S(1)} %fusion, f32[256,512,1,1]{0,1,3,2:T(8,128)S(1)} %bitcast.40, f32[64,2,256]{2,0,1:T(8,128)S(1)} %copy.24, f32[32,2,256]{2,1,0:T(2,128)S(1)} %copy.23, f32[64,2,256]{2,0,1:T(8,128)S(1)} %copy.22, f32[32,2,256]{2,1,0:T(2,128)S(1)} %copy.19), kind=kOutput, calls=%fused_computation.8 | convolution fusion | flops 6447693824 | bytes 17694720 | tf_op jit(solution)/shard_map/dot_general | solution.py:84
  71.4 10.6 %reshape.350 = f32[32,64,2,2,256]{4,3,1,2,0:T(2,128)} reshape(f32[32,64,2,512]{3,1,2,0:T(8,128)} %fusion.8) | data formatting | bytes 16777216 | tf_op jit(solution)/shard_map/reshape | solution.py:90
  81.9 8.0 %copy.29 = f32[32,64,2,2,256]{4,3,2,1,0:T(2,128)} copy(f32[32,64,2,2,256]{4,3,1,2,0:T(2,128)} %reshape.350) | data formatting | bytes 16777216 | tf_op jit(solution)/shard_map/reshape | solution.py:90
  (7 shorter events, 0.2 us)
Async XLA Ops:
  0.7 6.5 %collective-permute-start = (f32[2,192]{1,0:T(2,128)S(1)}, f32[2,192]{1,0:T(2,128)S(1)}, u32[]{:S(2)}, u32[]{:S(2)}) collective-permute-start(f32[2,192]{1,0:T(2,128)S(1)} %slice.43), channel_id=1, source_target_pairs={{1,0},{2,1},{3,2},{4,3},{5,4},{6,5},{7,6},{8,7},{9,8},{10,9},{11,1... | collective-permute-start | bytes 4616 | tf_op jit(solution)/shard_map/ppermute | solution.py:19
  9.9 12.1 %all-to-all-start = ((f32[8,1,1024]{2,1,0:T(1,128)}), f32[8,1,1024]{2,1,0:T(1,128)S(1)}, u32[]{:S(2)}, u32[]{:S(2)}) async-start(f32[8,1,1024]{2,1,0:T(1,128)} %reshape.367), calls=%async_computation | async-start | bytes 65536 | tf_op jit(solution)/shard_map/all_to_all | solution.py:104
  22.0 21.0 %all-to-all-start.1 = ((f32[4,1,2048]{2,1,0:T(1,128)}), f32[4,1,2048]{2,1,0:T(1,128)S(1)}, u32[]{:S(2)}, u32[]{:S(2)}) async-start(f32[4,1,2048]{2,1,0:T(1,128)} %reshape.365), calls=%async_computation.1 | async-start | bytes 65536 | tf_op jit(solution)/shard_map/all_to_all | solution.py:106
where the time goes:
time: 90.7 us; the launch traced here: 90 us
  blocking collectives  25 us (28%)
  local copies, waits for them, and re-layouts  23.8 us (26%)
  matrix products  18.3 us (20%)
  starting transfers between devices  11.8 us (13%)
  other arithmetic  5.47 us (6%)
  waiting for transfers between devices  5.31 us (6%)
    reshape x2, local copies, waits for them, and re-layouts, correlate(): return result.reshape(lead_count, trail_count, windows, 2, P_SIZE)  18.6 us
    all_gather x1, blocking collectives, local(): leading = lax.all_gather(leading, 'col', axis=3, tiled=True)  15.8 us
    dot_general x1, matrix products, correlate(): lax.dot_general(real_part, real_table, dims, precision=highest, preferred...  9.76 us
    all_gather x1, blocking collectives, local(): trailing = lax.all_gather(trailing, 'row', axis=2, tiled=True)  9.23 us
    dot_general x1, matrix products, correlate(): lax.dot_general(imag_part, imag_table, dims, precision=highest, preferred...  7.91 us
    all_to_all x1, starting transfers between devices, local(): lax.all_to_all(shaped, 'row', split_axis=1, concat_axis=2, tiled=True)  7.24 us
    all_to_all x1, waiting for transfers between devices, local(): lax.all_to_all(shaped, 'row', split_axis=1, concat_axis=2, tiled=True)  3.4 us
    all_to_all x1, starting transfers between devices, local(): lax.all_to_all(shaped, 'col', split_axis=1, concat_axis=3, tiled=True)  3.3 us
  transfers between devices with their start and end apart: 3, of which 2 were waited for; matrix products, arithmetic and copies ran while one was open for 7% of the time, Pallas kernels for 0%

commit v1 on v0

v1 whole, which is shorter than its diff:
```python
import functools
import math

import jax
import jax.numpy as jnp
import numpy as np
from jax import lax
from jax.experimental import pallas as pl
from jax.experimental.pallas import tpu as pltpu
from jax.sharding import PartitionSpec as P

C = 256
P_SIZE = 256
HOP = 64
LANES = 128
HALF = P_SIZE // 2
GROUP = 4


def split_table(table):
    high = table.astype(jnp.bfloat16)
    low = (table - high.astype(np.float64)).astype(jnp.bfloat16)
    return high, low


def channel_table():
    m = np.arange(C)
    hann = (0.5 - 0.5 * np.cos(2.0 * math.pi * m / C)) / math.sqrt(3.0 * C / 8.0)
    phase = 2.0 * math.pi * (np.arange(C)[:, None] * m[None, :] % C) / C
    cosine = hann * np.cos(phase)
    sinus = hann * np.sin(phase)
    upper = np.concatenate([cosine, sinus], axis=1)
    lower = np.concatenate([-sinus, cosine], axis=1)
    return np.stack([upper, lower])


def window_table(odd):
    p = 2 * np.arange(HALF) + odd
    phase = 2.0 * math.pi * (p[:, None] * np.arange(HALF)[None, :] % P_SIZE) / P_SIZE
    cosine = np.cos(phase) / math.sqrt(P_SIZE)
    sinus = np.sin(phase) / math.sqrt(P_SIZE)
    upper = np.concatenate([cosine, -sinus], axis=1)
    lower = np.concatenate([sinus, cosine], axis=1)
    return np.concatenate([upper, lower], axis=0)


def halves(x):
    high = x.astype(jnp.bfloat16)
    return high, (x - high.astype(jnp.float32)).astype(jnp.bfloat16)


def dot(a, b, contract=(1, 0)):
    return lax.dot_general(
        a,
        b,
        (((contract[0],), (contract[1],)), ((), ())),
        preferred_element_type=jnp.float32,
    )


def slot_of(index, order):
    return sum(((index >> bit) & 1) << stage for stage, bit in enumerate(order))


def kernel(order, sizes, key_ref, rec_ref, lead_ref, trail_ref, dft_ref, out_ref,
           real_ref, imag_ref, frame_ref, first_ref, second_ref, z_ref):
    devices, lead_width, trail_width, windows = sizes
    rows = devices * rec_ref.shape[1] // 2
    block = rec_ref.shape[1] // 2
    pattern = first_ref.shape[2]

    @pl.when(pl.program_id(0) == 0)
    def _():
        key = key_ref[0]
        for device in range(devices):
            slot = key ^ slot_of(device, order)
            piece = rec_ref[slot]
            real_ref[device * block : (device + 1) * block] = piece[:block]
            imag_ref[device * block : (device + 1) * block] = piece[block:]
        zeros = jnp.zeros((8, LANES), jnp.float32)
        real_ref[rows : rows + 8] = zeros
        imag_ref[rows : rows + 8] = zeros
        lower = lax.broadcasted_iota(jnp.int32, (HALF, LANES), 1) < HOP
        table = [jnp.concatenate([lead_ref[i, 0], lead_ref[i, 1], trail_ref[i, 0], trail_ref[i, 1]])
                 for i in range(2)]
        for window in range(windows):
            for part, ref in enumerate((real_ref, imag_ref)):
                shifts = [ref[window * HALF + i : window * HALF + i + HALF] for i in range(3)]
                turned = [pltpu.roll(x, HOP, 1) for x in shifts]
                odd = [jnp.where(lower, turned[i], turned[i + 1]) for i in range(2)]
                for start, pieces in ((0, shifts[:2]), (HALF, odd)):
                    for i, piece in enumerate(pieces):
                        high, low = halves(piece)
                        column = (2 * part + i) * LANES
                        frame_ref[0, start : start + HALF, column : column + LANES] = high
                        frame_ref[1, start : start + HALF, column : column + LANES] = low
            spectra = dot(table[0], frame_ref[0], (1, 1))
            spectra += dot(table[0], frame_ref[1], (1, 1))
            spectra += dot(table[1], frame_ref[0], (1, 1))
            start = 0
            for which, width in enumerate((lead_width, trail_width)):
                real = spectra[start : start + width]
                imag = spectra[start + width : start + 2 * width]
                start += 2 * width
                channel = lax.broadcasted_iota(jnp.int32, (width, HALF), 0)
                frame = lax.broadcasted_iota(jnp.int32, (width, HALF), 1)
                sign = jnp.where(channel & frame & 1 == 1, -1.0, 1.0)
                is_odd = channel & 1 == 1
                real_sign = jnp.where(channel & 3 >= 2, -sign, sign)
                imag_sign = jnp.where((channel + 1) & 3 >= 2, -sign, sign)
                values = (
                    real[:, :HALF] * sign,
                    imag[:, :HALF] * sign,
                    jnp.where(is_odd, imag[:, HALF:], real[:, HALF:]) * real_sign,
                    jnp.where(is_odd, real[:, HALF:], imag[:, HALF:]) * imag_sign,
                )
                for i, value in enumerate(values):
                    if which:
                        second_ref[i, pl.ds(window, width, stride=windows), :] = value
                    else:
                        for copy in range(pattern // windows):
                            first_ref[i, :, copy * windows + window, :] = value

    step = pl.program_id(0)
    height = trail_width * windows
    for local in range(GROUP):
        which = step * GROUP + local
        for start in range(0, height, pattern):
            lead = [first_ref[i, which] for i in range(4)]
            trail = [second_ref[i, start : start + pattern] for i in range(4)]
            for odd in range(2):
                ar, ai = lead[2 * odd : 2 * odd + 2]
                br, bi = trail[2 * odd : 2 * odd + 2]
                for part, value in enumerate((ar * br + ai * bi, ai * br - ar * bi)):
                    high, low = halves(value)
                    row = local * height + start
                    column = part * LANES
                    z_ref[odd, 0, row : row + pattern, column : column + LANES] = high
                    z_ref[odd, 1, row : row + pattern, column : column + LANES] = low
    chunk = min(256, height * GROUP)
    for row in range(0, height * GROUP, chunk):
        sums = []
        for odd in range(2):
            high = z_ref[odd, 0, row : row + chunk]
            low = z_ref[odd, 1, row : row + chunk]
            total = dot(high, dft_ref[odd, 0])
            total += dot(low, dft_ref[odd, 0])
            total += dot(high, dft_ref[odd, 1])
            sums.append(total)
        for i, value in enumerate((sums[0] + sums[1], sums[0] - sums[1])):
            for part in range(2):
                out_ref[pl.ds(row * 4 + 2 * i + part, chunk, stride=4), :] = value[
                    :, part * HALF : (part + 1) * HALF
                ]


def local(record):
    row_count = lax.axis_size("row")
    col_count = lax.axis_size("col")
    devices = row_count * col_count
    axes = ("row", "col")
    lead_width = C // row_count
    trail_width = C // col_count
    samples = record.shape[1]
    windows = samples * devices // HOP // P_SIZE
    row_index = lax.axis_index("row")
    col_index = lax.axis_index("col")
    me = row_index * col_count + col_index

    col_bits = list(range(col_count.bit_length() - 1))
    row_bits = list(range(len(col_bits), devices.bit_length() - 1))
    order = tuple(col_bits[::-1] + row_bits[1:] + row_bits[:1])
    blocks = record.reshape(1, 2 * samples // LANES, LANES)
    for bit in order:
        route = [(i, i ^ (1 << bit)) for i in range(devices)]
        blocks = jnp.concatenate([blocks, lax.ppermute(blocks, axes, route)], axis=0)

    table = jnp.asarray(np.stack(split_table(channel_table())))
    lead_table = lax.dynamic_slice_in_dim(table, row_index * lead_width, lead_width, 2)
    trail_table = lax.dynamic_slice_in_dim(table, col_index * trail_width, trail_width, 2)
    dft = jnp.asarray(np.stack([np.stack(split_table(window_table(odd))) for odd in range(2)]))
    key = slot_of(me, order).astype(jnp.int32).reshape(1)

    height = trail_width * windows
    pattern = max(8, windows)
    sizes = (devices, lead_width, trail_width, windows)
    vmem = pl.BlockSpec(memory_space=pltpu.VMEM)
    out = pl.pallas_call(
        functools.partial(kernel, order, sizes),
        grid=(lead_width // GROUP,),
        out_shape=jax.ShapeDtypeStruct((lead_width * height * 4, LANES), jnp.float32),
        in_specs=[pl.BlockSpec(memory_space=pltpu.SMEM), vmem, vmem, vmem, vmem],
        out_specs=pl.BlockSpec((GROUP * height * 4, LANES), lambda i: (i, 0)),
        scratch_shapes=[
            pltpu.VMEM((devices * samples // LANES + 8, LANES), jnp.float32),
            pltpu.VMEM((devices * samples // LANES + 8, LANES), jnp.float32),
            pltpu.VMEM((2, P_SIZE, 2 * C), jnp.bfloat16),
            pltpu.VMEM((4, lead_width, pattern, LANES), jnp.float32),
            pltpu.VMEM((4, height, LANES), jnp.float32),
            pltpu.VMEM((2, 2, GROUP * height, 2 * LANES), jnp.bfloat16),
        ],
        cost_estimate=pl.CostEstimate(flops=10**10, bytes_accessed=10**7, transcendentals=0),
    )(key, blocks, lead_table, trail_table, dft)
    out = out.reshape(lead_width, trail_width, windows, 2, 2, LANES)
    return out.transpose(0, 1, 2, 4, 3, 5).reshape(
        lead_width, trail_width, windows, 2, P_SIZE
    )


def solution(mesh):
    return jax.shard_map(
        local,
        mesh=mesh,
        in_specs=(P(None, ("row", "col")),),
        out_specs=P("row", "col", None, None, None),
        check_vma=False,
    )
```

time: 90.7 us -> 32.3 us (0.36)
  blocking collectives: 25 us -> 0 us
  local copies, waits for them, and re-layouts: 23.8 us -> 4.68 us
  matrix products: 18.3 us -> 0 us
  Pallas kernels: 0 us -> 9.67 us
  other arithmetic: 5.47 us -> 0.01 us
  waiting for transfers between devices: 5.31 us -> 7.95 us
  starting transfers between devices: 11.8 us -> 9.72 us
    all_gather x2 -> x0, blocking collectives: 25 us -> none  [the longest x1 15.8 us: local(): leading = lax.all_gather(leading, 'col', axis=3, tiled=True)]
    dot_general x3 -> x0, matrix products: 18.3 us -> none  [the longest x1 9.76 us: correlate(): lax.dot_general(real_part, real_table, dims, precision=highest, preferred...]
    reshape x4 -> x1, local copies, waits for them, and re-layouts: 18.8 us -> 0.71 us  [local(): blocks = record.reshape(1, 2 * samples // LANES, LANES)]
    all_to_all x2 -> x0, starting transfers between devices: 10.5 us -> none  [the longest x1 7.24 us: local(): lax.all_to_all(shaped, 'row', split_axis=1, concat_axis=2, tiled=True)]
    pallas_call x0 -> x1, Pallas kernels: none -> 9.67 us  [local(): pl.pallas_call(functools.partial(kernel, order, sizes), grid=(lead_width...]
    ppermute x1 -> x5, starting transfers between devices: 1.28 us -> 9.72 us  [local(): lax.ppermute(blocks, axes, route)]
    ppermute x1 -> x5, waiting for transfers between devices: 1.91 us -> 7.95 us  [local(): lax.ppermute(blocks, axes, route)]
    all_to_all x2 -> x0, waiting for transfers between devices: 3.4 us -> none  [the longest x1 3.4 us: local(): lax.all_to_all(shaped, 'row', split_axis=1, concat_axis=2, tiled=True)]
  transfers between devices with their start and end apart: 3 -> 5, of which waited for: 2 -> 4; matrix products, arithmetic and copies ran while one was open for 7% -> 10% of each run, Pallas kernels for 0% -> 0%
where the time goes in v1:
time: 32.3 us; the launch traced here: 32.1 us
  starting transfers between devices  9.72 us (30%)
  Pallas kernels  9.67 us (30%)
  waiting for transfers between devices  7.95 us (25%)
  local copies, waits for them, and re-layouts  4.68 us (14%)
    ppermute x5, starting transfers between devices, local(): lax.ppermute(blocks, axes, route)  9.72 us
    pallas_call x1, Pallas kernels, local(): pl.pallas_call(functools.partial(kernel, order, sizes), grid=(lead_width...  9.67 us
    ppermute x5, waiting for transfers between devices, local(): lax.ppermute(blocks, axes, route)  7.95 us
    dynamic_slice x1, local copies, waits for them, and re-layouts, local(): lax.dynamic_slice_in_dim(table, col_index * trail_width, trail_width, 2)  1.67 us
    dynamic_slice x1, local copies, waits for them, and re-layouts, local(): lax.dynamic_slice_in_dim(table, row_index * lead_width, lead_width, 2)  1.57 us
    unnamed x6, local copies, waits for them, and re-layouts  0.72 us
    reshape x1, local copies, waits for them, and re-layouts, local(): blocks = record.reshape(1, 2 * samples // LANES, LANES)  0.71 us
  transfers between devices with their start and end apart: 5, of which 4 were waited for; matrix products, arithmetic and copies ran while one was open for 10% of the time, Pallas kernels for 0%

profile of v1, /device:TPU:0, one launch (start us, length us, event | category | flops | bytes accessed | tf_op | source)
XLA Modules:
  0.0 32.1 jit_solution(53120789875837470)
XLA Ops:
  0.0 0.7 %reshape.13 = f32[1,16,128]{2,1,0:T(8,128)S(1)} reshape(f32[2,1024]{1,0:T(2,128)} %param.3) | data formatting | bytes 16384 | tf_op jit(solution)/shard_map/reshape | solution.py:173
  0.7 4.1 %collective-permute-start = (f32[1,16,128]{2,1,0:T(8,128)S(1)}, f32[1,16,128]{2,1,0:T(8,128)S(1)}, u32[]{:S(2)}, u32[]{:S(2)}) collective-permute-start(f32[1,16,128]{2,1,0:T(8,128)S(1)} %reshape.13), channel_id=1, source_target_pairs={{0,2},{1,3},{2,0},{3,1},{4,6},{5,7},{6,4},{7,5},{8,10},{9,11},{10,... | collective-permute-start | bytes 24584 | tf_op jit(solution)/shard_map/ppermute | solution.py:176
  4.8 1.6 %collective-permute-done = f32[1,16,128]{2,1,0:T(8,128)S(1)} collective-permute-done((f32[1,16,128]{2,1,0:T(8,128)S(1)}, f32[1,16,128]{2,1,0:T(8,128)S(1)}, u32[]{:S(2)}, u32[]{:S(2)}) %collective-permute-start) | collective-permute-done | bytes 8224 | tf_op jit(solution)/shard_map/ppermute | solution.py:176
  6.4 1.9 %collective-permute-start.1 = (f32[2,16,128]{2,1,0:T(8,128)S(1)}, f32[2,16,128]{2,1,0:T(8,128)S(1)}, u32[]{:S(2)}, u32[]{:S(2)}) collective-permute-start(f32[2,16,128]{2,1,0:T(8,128)S(1)} %pad_maximum_fusion.2), channel_id=1, source_target_pairs={{0,1},{1,0},{2,3},{3,2},{4,5},{5,4},{6,7},{7,6},{8,9},{9,8},{10,11... | collective-permute-start | bytes 49160 | tf_op jit(solution)/shard_map/ppermute | solution.py:176
  8.3 1.8 %collective-permute-done.1 = f32[2,16,128]{2,1,0:T(8,128)S(1)} collective-permute-done((f32[2,16,128]{2,1,0:T(8,128)S(1)}, f32[2,16,128]{2,1,0:T(8,128)S(1)}, u32[]{:S(2)}, u32[]{:S(2)}) %collective-permute-start.1) | collective-permute-done | bytes 16416 | tf_op jit(solution)/shard_map/ppermute | solution.py:176
  10.1 1.8 %collective-permute-start.2 = (f32[4,16,128]{2,1,0:T(8,128)S(1)}, f32[4,16,128]{2,1,0:T(8,128)S(1)}, u32[]{:S(2)}, u32[]{:S(2)}) collective-permute-start(f32[4,16,128]{2,1,0:T(8,128)S(1)} %pad_maximum_fusion.1), channel_id=1, source_target_pairs={{0,8},{1,9},{2,10},{3,11},{4,12},{5,13},{6,14},{7,15},{8,0},{9,1},... | collective-permute-start | bytes 98312 | tf_op jit(solution)/shard_map/ppermute | solution.py:176
  12.0 2.1 %collective-permute-done.2 = f32[4,16,128]{2,1,0:T(8,128)S(1)} collective-permute-done((f32[4,16,128]{2,1,0:T(8,128)S(1)}, f32[4,16,128]{2,1,0:T(8,128)S(1)}, u32[]{:S(2)}, u32[]{:S(2)}) %collective-permute-start.2) | collective-permute-done | bytes 32800 | tf_op jit(solution)/shard_map/ppermute | solution.py:176
  14.1 1.9 %collective-permute-start.3 = (f32[8,16,128]{2,1,0:T(8,128)S(1)}, f32[8,16,128]{2,1,0:T(8,128)S(1)}, u32[]{:S(2)}, u32[]{:S(2)}) collective-permute-start(f32[8,16,128]{2,1,0:T(8,128)S(1)} %pad_maximum_fusion), channel_id=1, source_target_pairs={{0,16},{1,17},{2,18},{3,19},{4,20},{5,21},{6,22},{7,23},{8,24},{9,... | collective-permute-start | bytes 196616 | tf_op jit(solution)/shard_map/ppermute | solution.py:176
  15.9 2.4 %collective-permute-done.3 = f32[8,16,128]{2,1,0:T(8,128)S(1)} collective-permute-done((f32[8,16,128]{2,1,0:T(8,128)S(1)}, f32[8,16,128]{2,1,0:T(8,128)S(1)}, u32[]{:S(2)}, u32[]{:S(2)}) %collective-permute-start.3) | collective-permute-done | bytes 65568 | tf_op jit(solution)/shard_map/ppermute | solution.py:176
  18.3 0.1 collective-permute-start.4
  18.4 1.6 %constant_dynamic-slice_fusion.1.lead_ref = bf16[2,2,32,512]{3,2,1,0:T(8,128)(2,1)} fusion(bf16[2,2,256,512]{3,2,1,0:T(8,128)(2,1)} %constant.29.clone, s32[]{:T(128)S(6)} %select_n.6), kind=kLoop, calls=%fused_computation.15 | loop fusion | bytes 262148 | tf_op jit(solution)/shard_map/dynamic_slice | solution.py:179
  20.0 1.7 %constant_dynamic-slice_fusion.trail_ref = bf16[2,2,64,512]{3,2,1,0:T(8,128)(2,1)} fusion(bf16[2,2,256,512]{3,2,1,0:T(8,128)(2,1)} %constant.29.clone, s32[]{:T(128)S(6)} %select_n.7), kind=kLoop, calls=%fused_computation.14 | loop fusion | bytes 524292 | tf_op jit(solution)/shard_map/dynamic_slice | solution.py:180
  21.7 0.0 collective-permute-done.4
  21.7 0.0 copy-start
  21.7 0.7 %copy-done = f32[32,16,128]{2,1,0:T(8,128)} copy-done((f32[32,16,128]{2,1,0:T(8,128)}, f32[32,16,128]{2,1,0:T(8,128)S(1)}, u32[]{:S(2)}) %copy-start) | copy-done | bytes 262168
  22.4 9.7 %shard_map.37 = f32[16384,128]{1,0:T(8,128)} custom-call(s32[1]{0:T(128)} %bitcast.key_ref, f32[32,16,128]{2,1,0:T(8,128)} %copy-done, bf16[2,2,32,512]{3,2,1,0:T(8,128)(2,1)} %constant_dynamic-slice_fusion.1.lead_ref, bf16[2,2,64,512]{3,2,1,0:T(8,128)(2,1)} %constant_dynamic-slice_fusion.trail_ref, bf16[2,2,256,256]{3,2,1,0:T(8,128)(2,1)} %constant.30.clone.dft_ref), custom_call_target="tpu_custom_call" | custom-call | flops 10000000000 | bytes 10000000 | tf_op jit(solution)/shard_map/pallas_call | solution.py:188
  (9 shorter events, 0.0 us)
Async XLA Ops:
  0.7 5.7 %collective-permute-start = (f32[1,16,128]{2,1,0:T(8,128)S(1)}, f32[1,16,128]{2,1,0:T(8,128)S(1)}, u32[]{:S(2)}, u32[]{:S(2)}) collective-permute-start(f32[1,16,128]{2,1,0:T(8,128)S(1)} %reshape.13), channel_id=1, source_target_pairs={{0,2},{1,3},{2,0},{3,1},{4,6},{5,7},{6,4},{7,5},{8,10},{9,11},{10,... | collective-permute-start | bytes 24584 | tf_op jit(solution)/shard_map/ppermute | solution.py:176
  6.4 3.7 %collective-permute-start.1 = (f32[2,16,128]{2,1,0:T(8,128)S(1)}, f32[2,16,128]{2,1,0:T(8,128)S(1)}, u32[]{:S(2)}, u32[]{:S(2)}) collective-permute-start(f32[2,16,128]{2,1,0:T(8,128)S(1)} %pad_maximum_fusion.2), channel_id=1, source_target_pairs={{0,1},{1,0},{2,3},{3,2},{4,5},{5,4},{6,7},{7,6},{8,9},{9,8},{10,11... | collective-permute-start | bytes 49160 | tf_op jit(solution)/shard_map/ppermute | solution.py:176
  10.1 3.9 %collective-permute-start.2 = (f32[4,16,128]{2,1,0:T(8,128)S(1)}, f32[4,16,128]{2,1,0:T(8,128)S(1)}, u32[]{:S(2)}, u32[]{:S(2)}) collective-permute-start(f32[4,16,128]{2,1,0:T(8,128)S(1)} %pad_maximum_fusion.1), channel_id=1, source_target_pairs={{0,8},{1,9},{2,10},{3,11},{4,12},{5,13},{6,14},{7,15},{8,0},{9,1},... | collective-permute-start | bytes 98312 | tf_op jit(solution)/shard_map/ppermute | solution.py:176
  14.1 4.3 %collective-permute-start.3 = (f32[8,16,128]{2,1,0:T(8,128)S(1)}, f32[8,16,128]{2,1,0:T(8,128)S(1)}, u32[]{:S(2)}, u32[]{:S(2)}) collective-permute-start(f32[8,16,128]{2,1,0:T(8,128)S(1)} %pad_maximum_fusion), channel_id=1, source_target_pairs={{0,16},{1,17},{2,18},{3,19},{4,20},{5,21},{6,22},{7,23},{8,24},{9,... | collective-permute-start | bytes 196616 | tf_op jit(solution)/shard_map/ppermute | solution.py:176
  18.3 3.3 %collective-permute-start.4 = (f32[16,16,128]{2,1,0:T(8,128)S(1)}, f32[16,16,128]{2,1,0:T(8,128)S(1)}, u32[]{:S(2)}, u32[]{:S(2)}) collective-permute-start(f32[16,16,128]{2,1,0:T(8,128)S(1)} %get-tuple-element.5), channel_id=1, source_target_pairs={{0,4},{1,5},{2,6},{3,7},{4,0},{5,1},{6,2},{7,3},{8,12},{9,13},{10,... | collective-permute-start | bytes 393224 | tf_op jit(solution)/shard_map/ppermute | solution.py:176
  21.7 0.7 %copy-start = (f32[32,16,128]{2,1,0:T(8,128)}, f32[32,16,128]{2,1,0:T(8,128)S(1)}, u32[]{:S(2)}) copy-start(f32[32,16,128]{2,1,0:T(8,128)S(1)} %constant_dynamic-update-slice_fusion.5.rec_ref) | copy-start | bytes 786436

commit v2 on v1

v2 whole, which is shorter than its diff:
```python
import functools
import math

import jax
import jax.numpy as jnp
import numpy as np
from jax import lax
from jax.experimental import pallas as pl
from jax.experimental.pallas import tpu as pltpu
from jax.sharding import PartitionSpec as P

C = 256
P_SIZE = 256
HOP = 64
LANES = 128
HALF = P_SIZE // 2
GROUP = 4


def split_table(table):
    high = table.astype(jnp.bfloat16)
    low = (table - high.astype(np.float64)).astype(jnp.bfloat16)
    return high, low


def channel_table():
    m = np.arange(C)
    hann = (0.5 - 0.5 * np.cos(2.0 * math.pi * m / C)) / math.sqrt(3.0 * C / 8.0)
    phase = 2.0 * math.pi * (np.arange(C)[:, None] * m[None, :] % C) / C
    cosine = hann * np.cos(phase)
    sinus = hann * np.sin(phase)
    upper = np.concatenate([cosine, sinus], axis=1)
    lower = np.concatenate([-sinus, cosine], axis=1)
    return np.stack([upper, lower])


def window_table(odd):
    p = 2 * np.arange(HALF) + odd
    phase = 2.0 * math.pi * (p[:, None] * np.arange(HALF)[None, :] % P_SIZE) / P_SIZE
    cosine = np.cos(phase) / math.sqrt(P_SIZE)
    sinus = np.sin(phase) / math.sqrt(P_SIZE)
    upper = np.concatenate([cosine, -sinus], axis=1)
    lower = np.concatenate([sinus, cosine], axis=1)
    return np.concatenate([upper, lower], axis=0)


def halves(x):
    high = x.astype(jnp.bfloat16)
    return high, (x - high.astype(jnp.float32)).astype(jnp.bfloat16)


def dot(a, b, contract=(1, 0)):
    return lax.dot_general(
        a,
        b,
        (((contract[0],), (contract[1],)), ((), ())),
        preferred_element_type=jnp.float32,
    )


def slot_of(index, order):
    return sum(((index >> bit) & 1) << stage for stage, bit in enumerate(order))


def fetch(widths, offset_ref, table_ref, dft_table_ref, weight_ref, dft_ref):
    start = 0
    for which, width in enumerate(widths):
        offset = pl.multiple_of(offset_ref[which], width)
        for part in range(2):
            for half in range(2):
                weight_ref[half, start : start + width] = table_ref[half, part, pl.ds(offset, width)]
            start += width
    dft_ref[...] = dft_table_ref[...]


def spectra_of(window, widths, real_ref, imag_ref, weight_ref, frame_ref):
    lower = lax.broadcasted_iota(jnp.int32, (HALF, LANES), 1) < HOP
    for part, ref in enumerate((real_ref, imag_ref)):
        shifts = [ref[window * HALF + i : window * HALF + i + HALF] for i in range(3)]
        turned = [pltpu.roll(x, HOP, 1) for x in shifts]
        odd = [jnp.where(lower, turned[i], turned[i + 1]) for i in range(2)]
        for start, pieces in ((0, shifts[:2]), (HALF, odd)):
            for i, piece in enumerate(pieces):
                high, low = halves(piece)
                column = (2 * part + i) * LANES
                frame_ref[0, start : start + HALF, column : column + LANES] = high
                frame_ref[1, start : start + HALF, column : column + LANES] = low
    spectra = dot(weight_ref[0], frame_ref[0], (1, 1))
    spectra += dot(weight_ref[0], frame_ref[1], (1, 1))
    spectra += dot(weight_ref[1], frame_ref[0], (1, 1))
    found = []
    start = 0
    for width in widths:
        real = spectra[start : start + width]
        imag = spectra[start + width : start + 2 * width]
        start += 2 * width
        channel = lax.broadcasted_iota(jnp.int32, (width, HALF), 0)
        frame = lax.broadcasted_iota(jnp.int32, (width, HALF), 1)
        sign = jnp.where(channel & frame & 1 == 1, -1.0, 1.0)
        is_odd = channel & 1 == 1
        real_sign = jnp.where(channel & 3 >= 2, -sign, sign)
        imag_sign = jnp.where((channel + 1) & 3 >= 2, -sign, sign)
        found.append((
            real[:, :HALF] * sign,
            imag[:, :HALF] * sign,
            jnp.where(is_odd, imag[:, HALF:], real[:, HALF:]) * real_sign,
            jnp.where(is_odd, real[:, HALF:], imag[:, HALF:]) * imag_sign,
        ))
    return found


def kernel(order, sizes, key_ref, rec_ref, weight_ref, dft_ref, out_ref,
           real_ref, imag_ref, frame_ref, first_ref, second_ref, even_ref, odd_ref, total_ref, sem):
    devices, widths, windows = sizes
    lead_width, trail_width = widths
    block = rec_ref.shape[1] // 2
    rows = devices * block
    pattern = first_ref.shape[1] // lead_width
    height = trail_width * windows
    steps = lead_width // GROUP

    key = key_ref[0]
    for device in range(devices):
        slot = key ^ slot_of(device, order)
        piece = rec_ref[slot]
        real_ref[device * block : (device + 1) * block] = piece[:block]
        imag_ref[device * block : (device + 1) * block] = piece[block:]
    zeros = jnp.zeros((8, LANES), jnp.float32)
    real_ref[rows : rows + 8] = zeros
    imag_ref[rows : rows + 8] = zeros
    for window in range(windows):
        lead, trail = spectra_of(window, widths, real_ref, imag_ref, weight_ref, frame_ref)
        for i in range(4):
            second_ref[i, pl.ds(window, trail_width, stride=windows), :] = trail[i]
            for copy in range(pattern // windows):
                place = pl.ds(copy * windows + window, lead_width, stride=pattern)
                first_ref[i, place, :] = lead[i]

    def multiply(step, z_ref):
        for local in range(GROUP):
            place = pl.ds(pl.multiple_of((step * GROUP + local) * pattern, pattern), pattern)
            lead = [first_ref[i, place, :] for i in range(4)]
            for start in range(0, height, pattern):
                trail = [second_ref[i, start : start + pattern] for i in range(4)]
                row = local * height + start
                for odd in range(2):
                    ar, ai = lead[2 * odd : 2 * odd + 2]
                    br, bi = trail[2 * odd : 2 * odd + 2]
                    for part, value in enumerate((ar * br + ai * bi, ai * br - ar * bi)):
                        high, low = halves(value)
                        column = part * LANES
                        z_ref[odd, 0, row : row + pattern, column : column + LANES] = high
                        z_ref[odd, 1, row : row + pattern, column : column + LANES] = low

    def copy_out(step):
        size = GROUP * height * 4
        place = pl.ds(pl.multiple_of(step * size, size), size)
        return pltpu.make_async_copy(total_ref.at[place], out_ref.at[place], sem.at[step])

    def transform(step, z_ref):
        chunk = min(256, height * GROUP)
        for row in range(0, height * GROUP, chunk):
            sums = []
            for odd in range(2):
                high = z_ref[odd, 0, row : row + chunk]
                low = z_ref[odd, 1, row : row + chunk]
                total = dot(high, dft_ref[odd, 0])
                total += dot(low, dft_ref[odd, 0])
                total += dot(high, dft_ref[odd, 1])
                sums.append(total)
            base = pl.multiple_of((step * GROUP * height + row) * 4, 4 * chunk)
            for i, value in enumerate((sums[0] + sums[1], sums[0] - sums[1])):
                for part in range(2):
                    total_ref[pl.ds(base + 2 * i + part, chunk, stride=4), :] = value[
                        :, part * HALF : (part + 1) * HALF
                    ]
        copy_out(step).start()

    multiply(0, even_ref)

    @pl.loop(0, steps, step=2)
    def _(step):
        multiply(step + 1, odd_ref)
        transform(step, even_ref)
        multiply(jnp.minimum(step + 2, steps - 1), even_ref)
        transform(step + 1, odd_ref)

    for step in range(steps):
        copy_out(step).wait()


def tables(widths, offsets):
    table = jnp.asarray(np.stack(split_table(channel_table())))
    dft = jnp.asarray(np.stack([np.stack(split_table(window_table(odd))) for odd in range(2)]))
    vmem = pl.BlockSpec(memory_space=pltpu.VMEM)
    return pl.pallas_call(
        functools.partial(fetch, widths),
        out_shape=(
            jax.ShapeDtypeStruct((2, 2 * sum(widths), 2 * C), jnp.bfloat16),
            jax.ShapeDtypeStruct(dft.shape, jnp.bfloat16),
        ),
        in_specs=[pl.BlockSpec(memory_space=pltpu.SMEM), vmem, vmem],
        out_specs=(vmem, vmem),
        compiler_params=pltpu.CompilerParams(vmem_limit_bytes=8 * 2**20),
        cost_estimate=pl.CostEstimate(flops=2 * 10**9, bytes_accessed=10**6, transcendentals=0),
    )(offsets, table, dft)


def local(record):
    row_count = lax.axis_size("row")
    col_count = lax.axis_size("col")
    devices = row_count * col_count
    axes = ("row", "col")
    lead_width = C // row_count
    trail_width = C // col_count
    samples = record.shape[1]
    windows = samples * devices // HOP // P_SIZE
    row_index = lax.axis_index("row")
    col_index = lax.axis_index("col")
    me = row_index * col_count + col_index

    col_bits = list(range(col_count.bit_length() - 1))
    row_bits = list(range(len(col_bits), devices.bit_length() - 1))
    order = tuple(col_bits[::-1] + row_bits[1:] + row_bits[:1])
    widths = (lead_width, trail_width)
    offsets = jnp.stack([row_index * lead_width, col_index * trail_width]).astype(jnp.int32)
    weights, dft = tables(widths, offsets)
    blocks = record.reshape(1, 2 * samples // LANES, LANES)
    for stage, bit in enumerate(order):
        if stage == 1:
            blocks, weights, dft = lax.optimization_barrier((blocks, weights, dft))
        route = [(i, i ^ (1 << bit)) for i in range(devices)]
        blocks = jnp.concatenate([blocks, lax.ppermute(blocks, axes, route)], axis=0)

    key = slot_of(me, order).astype(jnp.int32).reshape(1)
    height = trail_width * windows
    pattern = max(8, windows)
    sizes = (devices, widths, windows)
    vmem = pl.BlockSpec(memory_space=pltpu.VMEM)
    smem = pl.BlockSpec(memory_space=pltpu.SMEM)
    out = pl.pallas_call(
        functools.partial(kernel, order, sizes),
        out_shape=jax.ShapeDtypeStruct((lead_width * height * 4, LANES), jnp.float32),
        in_specs=[smem, vmem, vmem, vmem],
        out_specs=pl.BlockSpec(memory_space=pltpu.HBM),
        scratch_shapes=[
            pltpu.VMEM((devices * samples // LANES + 8, LANES), jnp.float32),
            pltpu.VMEM((devices * samples // LANES + 8, LANES), jnp.float32),
            pltpu.VMEM((2, P_SIZE, 2 * C), jnp.bfloat16),
            pltpu.VMEM((4, lead_width * pattern, LANES), jnp.float32),
            pltpu.VMEM((4, height, LANES), jnp.float32),
            pltpu.VMEM((2, 2, GROUP * height, 2 * LANES), jnp.bfloat16),
            pltpu.VMEM((2, 2, GROUP * height, 2 * LANES), jnp.bfloat16),
            pltpu.VMEM((lead_width * height * 4, LANES), jnp.float32),
            pltpu.SemaphoreType.DMA((lead_width // GROUP,)),
        ],
        compiler_params=pltpu.CompilerParams(vmem_limit_bytes=40 * 2**20),
        cost_estimate=pl.CostEstimate(flops=10**10, bytes_accessed=10**7, transcendentals=0),
    )(key, blocks, weights, dft)
    out = out.reshape(lead_width, trail_width, windows, 2, 2, LANES)
    return out.transpose(0, 1, 2, 4, 3, 5).reshape(
        lead_width, trail_width, windows, 2, P_SIZE
    )


def solution(mesh):
    return jax.shard_map(
        local,
        mesh=mesh,
        in_specs=(P(None, ("row", "col")),),
        out_specs=P("row", "col", None, None, None),
        check_vma=False,
    )
```

time: 32.3 us -> 28 us (0.87)
  Pallas kernels: 9.67 us -> 7.23 us
  local copies, waits for them, and re-layouts: 4.68 us -> 3 us
  starting transfers between devices: 9.72 us -> 8.79 us
  waiting for transfers between devices: 7.95 us -> 8.64 us
    dynamic_slice x2 -> x0, local copies, waits for them, and re-layouts: 3.24 us -> none  [the longest x1 1.67 us: local(): lax.dynamic_slice_in_dim(table, col_index * trail_width, trail_width, 2)]
    pallas_call x1 -> x2, Pallas kernels: 9.67 us -> 7.23 us  [the longest x1 6.63 us: local(): pl.pallas_call(functools.partial(kernel, order, sizes), out_shape=jax.Sha...]
    unnamed x6 -> x8, local copies, waits for them, and re-layouts: 0.72 us -> 2.28 us
    ppermute x5, starting transfers between devices: 9.72 us -> 8.79 us  [local(): lax.ppermute(blocks, axes, route)]
    ppermute x5, waiting for transfers between devices: 7.95 us -> 8.64 us  [local(): lax.ppermute(blocks, axes, route)]
  transfers between devices with their start and end apart: 5 -> 5, of which waited for: 4 -> 4; matrix products, arithmetic and copies ran while one was open for 10% -> 0% of each run, Pallas kernels for 0% -> 2%
where the time goes in v2:
time: 28 us; the launch traced here: 27.8 us
  starting transfers between devices  8.79 us (31%)
  waiting for transfers between devices  8.64 us (31%)
  Pallas kernels  7.23 us (26%)
  local copies, waits for them, and re-layouts  3 us (11%)
    ppermute x5, starting transfers between devices, local(): lax.ppermute(blocks, axes, route)  8.79 us
    ppermute x5, waiting for transfers between devices, local(): lax.ppermute(blocks, axes, route)  8.64 us
    pallas_call x1, Pallas kernels, local(): pl.pallas_call(functools.partial(kernel, order, sizes), out_shape=jax.Sha...  6.63 us
    unnamed x8, local copies, waits for them, and re-layouts  2.28 us
    reshape x1, local copies, waits for them, and re-layouts, local(): blocks = record.reshape(1, 2 * samples // LANES, LANES)  0.71 us
    pallas_call x1, Pallas kernels, tables(): pl.pallas_call(functools.partial(fetch, widths), out_shape=(jax.ShapeDtyp...  0.6 us
  transfers between devices with their start and end apart: 5, of which 4 were waited for; matrix products, arithmetic and copies ran while one was open for 0% of the time, Pallas kernels for 2%

profile of v2, /device:TPU:0, one launch (start us, length us, event | category | flops | bytes accessed | tf_op | source)
XLA Modules:
  0.0 27.8 jit_solution(14840490147507596029)
XLA Ops:
  0.0 0.7 %reshape.13 = f32[1,16,128]{2,1,0:T(8,128)S(1)} reshape(f32[2,1024]{1,0:T(2,128)} %param.3) | data formatting | bytes 16384 | tf_op jit(solution)/shard_map/reshape | solution.py:228
  0.7 4.1 %collective-permute-start = (f32[1,16,128]{2,1,0:T(8,128)S(1)}, f32[1,16,128]{2,1,0:T(8,128)S(1)}, u32[]{:S(2)}, u32[]{:S(2)}) collective-permute-start(f32[1,16,128]{2,1,0:T(8,128)S(1)} %reshape.13), channel_id=1, source_target_pairs={{0,2},{1,3},{2,0},{3,1},{4,6},{5,7},{6,4},{7,5},{8,10},{9,11},{10,... | collective-permute-start | bytes 24584 | tf_op jit(solution)/shard_map/ppermute | solution.py:233
  4.8 0.1 pad_add_fusion.offset_ref
  4.8 0.0 copy-start
  4.8 1.2 %copy-done = bf16[2,2,256,512]{3,2,1,0:T(8,128)(2,1)S(1)} copy-done((bf16[2,2,256,512]{3,2,1,0:T(8,128)(2,1)S(1)}, bf16[2,2,256,512]{3,2,1,0:T(8,128)(2,1)}, u32[]{:S(2)}) %copy-start) | copy-done | bytes 1048600
  6.1 0.0 copy-start.1
  6.1 1.0 %copy-done.1 = bf16[2,2,256,256]{3,2,1,0:T(8,128)(2,1)S(1)} copy-done((bf16[2,2,256,256]{3,2,1,0:T(8,128)(2,1)S(1)}, bf16[2,2,256,256]{3,2,1,0:T(8,128)(2,1)}, u32[]{:S(2)}) %copy-start.1) | copy-done | bytes 524312
  7.1 0.6 %shard_map.37 = (bf16[2,192,512]{2,1,0:T(8,128)(2,1)S(1)}, bf16[2,2,256,256]{3,2,1,0:T(8,128)(2,1)S(1)}) custom-call(s32[2]{0:T(128)S(1)} %pad_add_fusion.offset_ref, bf16[2,2,256,512]{3,2,1,0:T(8,128)(2,1)S(1)} %copy-done, bf16[2,2,256,256]{3,2,1,0:T(8,128)(2,1)S(1)} %copy-done.1), custom_call_target="tpu_custom_call" | custom-call | flops 2000000000 | bytes 1000000 | tf_op jit(solution)/shard_map/pallas_call | solution.py:196
  7.7 0.0 collective-permute-done
  7.7 1.6 %collective-permute-start.1 = (f32[2,16,128]{2,1,0:T(8,128)S(1)}, f32[2,16,128]{2,1,0:T(8,128)S(1)}, u32[]{:S(2)}, u32[]{:S(2)}) collective-permute-start(f32[2,16,128]{2,1,0:T(8,128)S(1)} %pad_maximum_fusion.3), channel_id=1, source_target_pairs={{0,1},{1,0},{2,3},{3,2},{4,5},{5,4},{6,7},{7,6},{8,9},{9,8},{10,11... | collective-permute-start | bytes 49160 | tf_op jit(solution)/shard_map/ppermute | solution.py:233
  9.4 2.2 %collective-permute-done.1 = f32[2,16,128]{2,1,0:T(8,128)S(1)} collective-permute-done((f32[2,16,128]{2,1,0:T(8,128)S(1)}, f32[2,16,128]{2,1,0:T(8,128)S(1)}, u32[]{:S(2)}, u32[]{:S(2)}) %collective-permute-start.1) | collective-permute-done | bytes 16416 | tf_op jit(solution)/shard_map/ppermute | solution.py:233
  11.6 1.5 %collective-permute-start.2 = (f32[4,16,128]{2,1,0:T(8,128)S(1)}, f32[4,16,128]{2,1,0:T(8,128)S(1)}, u32[]{:S(2)}, u32[]{:S(2)}) collective-permute-start(f32[4,16,128]{2,1,0:T(8,128)S(1)} %pad_maximum_fusion.2), channel_id=1, source_target_pairs={{0,8},{1,9},{2,10},{3,11},{4,12},{5,13},{6,14},{7,15},{8,0},{9,1},... | collective-permute-start | bytes 98312 | tf_op jit(solution)/shard_map/ppermute | solution.py:233
  13.0 2.4 %collective-permute-done.2 = f32[4,16,128]{2,1,0:T(8,128)S(1)} collective-permute-done((f32[4,16,128]{2,1,0:T(8,128)S(1)}, f32[4,16,128]{2,1,0:T(8,128)S(1)}, u32[]{:S(2)}, u32[]{:S(2)}) %collective-permute-start.2) | collective-permute-done | bytes 32800 | tf_op jit(solution)/shard_map/ppermute | solution.py:233
  15.5 1.5 %collective-permute-start.3 = (f32[8,16,128]{2,1,0:T(8,128)S(1)}, f32[8,16,128]{2,1,0:T(8,128)S(1)}, u32[]{:S(2)}, u32[]{:S(2)}) collective-permute-start(f32[8,16,128]{2,1,0:T(8,128)S(1)} %pad_maximum_fusion.1), channel_id=1, source_target_pairs={{0,16},{1,17},{2,18},{3,19},{4,20},{5,21},{6,22},{7,23},{8,24},{9,... | collective-permute-start | bytes 196616 | tf_op jit(solution)/shard_map/ppermute | solution.py:233
  17.0 2.7 %collective-permute-done.3 = f32[8,16,128]{2,1,0:T(8,128)S(1)} collective-permute-done((f32[8,16,128]{2,1,0:T(8,128)S(1)}, f32[8,16,128]{2,1,0:T(8,128)S(1)}, u32[]{:S(2)}, u32[]{:S(2)}) %collective-permute-start.3) | collective-permute-done | bytes 65568 | tf_op jit(solution)/shard_map/ppermute | solution.py:233
  19.8 0.1 collective-permute-start.4
  19.9 1.3 %collective-permute-done.4 = f32[16,16,128]{2,1,0:T(8,128)S(1)} collective-permute-done((f32[16,16,128]{2,1,0:T(8,128)S(1)}, f32[16,16,128]{2,1,0:T(8,128)S(1)}, u32[]{:S(2)}, u32[]{:S(2)}) %collective-permute-start.4) | collective-permute-done | bytes 131104 | tf_op jit(solution)/shard_map/ppermute | solution.py:233
  21.2 6.6 %shard_map.38 = f32[16384,128]{1,0:T(8,128)} custom-call(s32[1]{0:T(128)} %bitcast.key_ref, f32[32,16,128]{2,1,0:T(8,128)S(1)} %constant_dynamic-update-slice_fusion.rec_ref, bf16[2,192,512]{2,1,0:T(8,128)(2,1)S(1)} %get-tuple-element.13.weight_ref, bf16[2,2,256,256]{3,2,1,0:T(8,128)(2,1)S(1)} %get-tuple-element.14.dft_ref), custom_call_target="tpu_custom_call" | custom-call | flops 10000000000 | bytes 10000000 | tf_op jit(solution)/shard_map/pallas_call | solution.py:241
  (9 shorter events, 0.0 us)
Async XLA Ops:
  0.7 7.0 %collective-permute-start = (f32[1,16,128]{2,1,0:T(8,128)S(1)}, f32[1,16,128]{2,1,0:T(8,128)S(1)}, u32[]{:S(2)}, u32[]{:S(2)}) collective-permute-start(f32[1,16,128]{2,1,0:T(8,128)S(1)} %reshape.13), channel_id=1, source_target_pairs={{0,2},{1,3},{2,0},{3,1},{4,6},{5,7},{6,4},{7,5},{8,10},{9,11},{10,... | collective-permute-start | bytes 24584 | tf_op jit(solution)/shard_map/ppermute | solution.py:233
  4.8 1.2 %copy-start = (bf16[2,2,256,512]{3,2,1,0:T(8,128)(2,1)S(1)}, bf16[2,2,256,512]{3,2,1,0:T(8,128)(2,1)}, u32[]{:S(2)}) copy-start(bf16[2,2,256,512]{3,2,1,0:T(8,128)(2,1)} %constant.27.clone.table_ref) | copy-start | bytes 3145732
  6.1 1.0 %copy-start.1 = (bf16[2,2,256,256]{3,2,1,0:T(8,128)(2,1)S(1)}, bf16[2,2,256,256]{3,2,1,0:T(8,128)(2,1)}, u32[]{:S(2)}) copy-start(bf16[2,2,256,256]{3,2,1,0:T(8,128)(2,1)} %constant.28.clone.dft_table_ref) | copy-start | bytes 1572868
  7.7 3.8 %collective-permute-start.1 = (f32[2,16,128]{2,1,0:T(8,128)S(1)}, f32[2,16,128]{2,1,0:T(8,128)S(1)}, u32[]{:S(2)}, u32[]{:S(2)}) collective-permute-start(f32[2,16,128]{2,1,0:T(8,128)S(1)} %pad_maximum_fusion.3), channel_id=1, source_target_pairs={{0,1},{1,0},{2,3},{3,2},{4,5},{5,4},{6,7},{7,6},{8,9},{9,8},{10,11... | collective-permute-start | bytes 49160 | tf_op jit(solution)/shard_map/ppermute | solution.py:233
  11.6 3.9 %collective-permute-start.2 = (f32[4,16,128]{2,1,0:T(8,128)S(1)}, f32[4,16,128]{2,1,0:T(8,128)S(1)}, u32[]{:S(2)}, u32[]{:S(2)}) collective-permute-start(f32[4,16,128]{2,1,0:T(8,128)S(1)} %pad_maximum_fusion.2), channel_id=1, source_target_pairs={{0,8},{1,9},{2,10},{3,11},{4,12},{5,13},{6,14},{7,15},{8,0},{9,1},... | collective-permute-start | bytes 98312 | tf_op jit(solution)/shard_map/ppermute | solution.py:233
  15.5 4.3 %collective-permute-start.3 = (f32[8,16,128]{2,1,0:T(8,128)S(1)}, f32[8,16,128]{2,1,0:T(8,128)S(1)}, u32[]{:S(2)}, u32[]{:S(2)}) collective-permute-start(f32[8,16,128]{2,1,0:T(8,128)S(1)} %pad_maximum_fusion.1), channel_id=1, source_target_pairs={{0,16},{1,17},{2,18},{3,19},{4,20},{5,21},{6,22},{7,23},{8,24},{9,... | collective-permute-start | bytes 196616 | tf_op jit(solution)/shard_map/ppermute | solution.py:233
  19.8 1.4 %collective-permute-start.4 = (f32[16,16,128]{2,1,0:T(8,128)S(1)}, f32[16,16,128]{2,1,0:T(8,128)S(1)}, u32[]{:S(2)}, u32[]{:S(2)}) collective-permute-start(f32[16,16,128]{2,1,0:T(8,128)S(1)} %pad_maximum_fusion), channel_id=1, source_target_pairs={{0,4},{1,5},{2,6},{3,7},{4,0},{5,1},{6,2},{7,3},{8,12},{9,13},{10,... | collective-permute-start | bytes 393224 | tf_op jit(solution)/shard_map/ppermute | solution.py:233

commit v3 on v2

--- a/solution.py
+++ b/solution.py
@@ -62,15 +62,30 @@
     return sum(((index >> bit) & 1) << stage for stage, bit in enumerate(order))
 
 
-def fetch(widths, offset_ref, table_ref, dft_table_ref, weight_ref, dft_ref):
+def fetch_weights(widths, offset_ref, table_ref, weight_ref, sem):
+    copies = []
     start = 0
     for which, width in enumerate(widths):
         offset = pl.multiple_of(offset_ref[which], width)
         for part in range(2):
-            for half in range(2):
-                weight_ref[half, start : start + width] = table_ref[half, part, pl.ds(offset, width)]
+            copies.append(
+                pltpu.make_async_copy(
+                    table_ref.at[:, part, pl.ds(offset, width)],
+                    weight_ref.at[:, pl.ds(start, width)],
+                    sem.at[len(copies)],
+                )
+            )
             start += width
-    dft_ref[...] = dft_table_ref[...]
+    for copy in copies:
+        copy.start()
+    for copy in copies:
+        copy.wait()
+
+
+def fetch_whole(table_ref, copy_ref, sem):
+    copy = pltpu.make_async_copy(table_ref, copy_ref, sem)
+    copy.start()
+    copy.wait()
 
 
 def spectra_of(window, widths, real_ref, imag_ref, weight_ref, frame_ref):
@@ -189,21 +204,17 @@
         copy_out(step).wait()
 
 
-def tables(widths, offsets):
-    table = jnp.asarray(np.stack(split_table(channel_table())))
-    dft = jnp.asarray(np.stack([np.stack(split_table(window_table(odd))) for odd in range(2)]))
-    vmem = pl.BlockSpec(memory_space=pltpu.VMEM)
+def fetched(body, scalars, table, shape, sem):
     return pl.pallas_call(
-        functools.partial(fetch, widths),
-        out_shape=(
-            jax.ShapeDtypeStruct((2, 2 * sum(widths), 2 * C), jnp.bfloat16),
-            jax.ShapeDtypeStruct(dft.shape, jnp.bfloat16),
-        ),
-        in_specs=[pl.BlockSpec(memory_space=pltpu.SMEM), vmem, vmem],
-        out_specs=(vmem, vmem),
+        body,
+        out_shape=jax.ShapeDtypeStruct(shape, table.dtype),
+        in_specs=[pl.BlockSpec(memory_space=pltpu.SMEM)] * len(scalars)
+        + [pl.BlockSpec(memory_space=pltpu.HBM)],
+        out_specs=pl.BlockSpec(memory_space=pltpu.VMEM),
+        scratch_shapes=[sem],
         compiler_params=pltpu.CompilerParams(vmem_limit_bytes=8 * 2**20),
-        cost_estimate=pl.CostEstimate(flops=2 * 10**9, bytes_accessed=10**6, transcendentals=0),
-    )(offsets, table, dft)
+        cost_estimate=pl.CostEstimate(flops=10**9, bytes_accessed=10**6, transcendentals=0),
+    )(*scalars, pltpu.with_memory_space_constraint(jnp.asarray(table), pltpu.HBM))
 
 
 def local(record):
@@ -224,11 +235,21 @@
     order = tuple(col_bits[::-1] + row_bits[1:] + row_bits[:1])
     widths = (lead_width, trail_width)
     offsets = jnp.stack([row_index * lead_width, col_index * trail_width]).astype(jnp.int32)
-    weights, dft = tables(widths, offsets)
+    weights = fetched(
+        functools.partial(fetch_weights, widths),
+        (offsets,),
+        np.stack(split_table(channel_table())),
+        (2, 2 * sum(widths), 2 * C),
+        pltpu.SemaphoreType.DMA((4,)),
+    )
+    dft = np.stack([np.stack(split_table(window_table(odd))) for odd in range(2)])
+    dft = fetched(fetch_whole, (), dft, dft.shape, pltpu.SemaphoreType.DMA(()))
     blocks = record.reshape(1, 2 * samples // LANES, LANES)
     for stage, bit in enumerate(order):
         if stage == 1:
-            blocks, weights, dft = lax.optimization_barrier((blocks, weights, dft))
+            blocks, weights = lax.optimization_barrier((blocks, weights))
+        if stage == 2:
+            blocks, dft = lax.optimization_barrier((blocks, dft))
         route = [(i, i ^ (1 << bit)) for i in range(devices)]
         blocks = jnp.concatenate([blocks, lax.ppermute(blocks, axes, route)], axis=0)
 

time: 28 us -> 26.8 us (0.957)
  local copies, waits for them, and re-layouts: 3 us -> 0.71 us
  Pallas kernels: 7.23 us -> 9.3 us
  waiting for transfers between devices: 8.64 us -> 7.07 us
  starting transfers between devices: 8.79 us -> 9.32 us
    unnamed x8 -> x0, local copies, waits for them, and re-layouts: 2.28 us -> none
    pallas_call x1 -> x2, Pallas kernels: 0.6 us -> 2.67 us  [fetched(): pl.pallas_call(body, out_shape=jax.ShapeDtypeStruct(shape, table.dtype),...]
    ppermute x5, waiting for transfers between devices: 8.64 us -> 7.07 us  [local(): lax.ppermute(blocks, axes, route)]
    ppermute x5, starting transfers between devices: 8.79 us -> 9.32 us  [local(): lax.ppermute(blocks, axes, route)]
  transfers between devices with their start and end apart: 5 -> 5, of which waited for: 4 -> 4; matrix products, arithmetic and copies ran while one was open for 0% -> 0% of each run, Pallas kernels for 2% -> 10%
where the time goes in v3:
time: 26.8 us; the launch traced here: 26.6 us
  starting transfers between devices  9.32 us (35%)
  Pallas kernels  9.3 us (35%)
  waiting for transfers between devices  7.07 us (26%)
  local copies, waits for them, and re-layouts  0.71 us (3%)
    ppermute x5, starting transfers between devices, local(): lax.ppermute(blocks, axes, route)  9.32 us
    ppermute x5, waiting for transfers between devices, local(): lax.ppermute(blocks, axes, route)  7.07 us
    pallas_call x1, Pallas kernels, local(): pl.pallas_call(functools.partial(kernel, order, sizes), out_shape=jax.Sha...  6.63 us
    pallas_call x2, Pallas kernels, fetched(): pl.pallas_call(body, out_shape=jax.ShapeDtypeStruct(shape, table.dtype),...  2.67 us
    reshape x1, local copies, waits for them, and re-layouts, local(): blocks = record.reshape(1, 2 * samples // LANES, LANES)  0.71 us
  transfers between devices with their start and end apart: 5, of which 4 were waited for; matrix products, arithmetic and copies ran while one was open for 0% of the time, Pallas kernels for 10%

profile of v3, /device:TPU:0, one launch (start us, length us, event | category | flops | bytes accessed | tf_op | source)
XLA Modules:
  0.0 26.6 jit_solution(15443665387450182182)
XLA Ops:
  0.0 0.7 %reshape.13 = f32[1,16,128]{2,1,0:T(8,128)S(1)} reshape(f32[2,1024]{1,0:T(2,128)} %param.3) | data formatting | bytes 16384 | tf_op jit(solution)/shard_map/reshape | solution.py:247
  0.7 4.1 %collective-permute-start = (f32[1,16,128]{2,1,0:T(8,128)S(1)}, f32[1,16,128]{2,1,0:T(8,128)S(1)}, u32[]{:S(2)}, u32[]{:S(2)}) collective-permute-start(f32[1,16,128]{2,1,0:T(8,128)S(1)} %reshape.13), channel_id=1, source_target_pairs={{0,2},{1,3},{2,0},{3,1},{4,6},{5,7},{6,4},{7,5},{8,10},{9,11},{10,... | collective-permute-start | bytes 24584 | tf_op jit(solution)/shard_map/ppermute | solution.py:254
  4.8 0.1 pad_add_fusion.offset_ref
  4.8 1.6 %shard_map.37.weight_ref = bf16[2,192,512]{2,1,0:T(8,128)(2,1)S(1)} custom-call(s32[2]{0:T(128)S(1)} %pad_add_fusion.offset_ref, bf16[2,2,256,512]{3,2,1,0:T(8,128)(2,1)} %constant.27.clone.table_ref), custom_call_target="tpu_custom_call" | custom-call | flops 1000000000 | bytes 1000000 | tf_op jit(solution)/shard_map/pallas_call | solution.py:208
  6.5 0.0 collective-permute-done
  6.5 1.8 %collective-permute-start.1 = (f32[2,16,128]{2,1,0:T(8,128)S(1)}, f32[2,16,128]{2,1,0:T(8,128)S(1)}, u32[]{:S(2)}, u32[]{:S(2)}) collective-permute-start(f32[2,16,128]{2,1,0:T(8,128)S(1)} %pad_maximum_fusion.4), channel_id=1, source_target_pairs={{0,1},{1,0},{2,3},{3,2},{4,5},{5,4},{6,7},{7,6},{8,9},{9,8},{10,11... | collective-permute-start | bytes 49160 | tf_op jit(solution)/shard_map/ppermute | solution.py:254
  8.3 1.0 %shard_map.38.dft_ref = bf16[2,2,256,256]{3,2,1,0:T(8,128)(2,1)S(1)} custom-call(bf16[2,2,256,256]{3,2,1,0:T(8,128)(2,1)} %constant.28.clone.table_ref), custom_call_target="tpu_custom_call" | custom-call | flops 1000000000 | bytes 1000000 | tf_op jit(solution)/shard_map/pallas_call | solution.py:208
  9.4 0.9 %collective-permute-done.1 = f32[2,16,128]{2,1,0:T(8,128)S(1)} collective-permute-done((f32[2,16,128]{2,1,0:T(8,128)S(1)}, f32[2,16,128]{2,1,0:T(8,128)S(1)}, u32[]{:S(2)}, u32[]{:S(2)}) %collective-permute-start.1) | collective-permute-done | bytes 16416 | tf_op jit(solution)/shard_map/ppermute | solution.py:254
  10.3 1.7 %collective-permute-start.2 = (f32[4,16,128]{2,1,0:T(8,128)S(1)}, f32[4,16,128]{2,1,0:T(8,128)S(1)}, u32[]{:S(2)}, u32[]{:S(2)}) collective-permute-start(f32[4,16,128]{2,1,0:T(8,128)S(1)} %pad_maximum_fusion.3), channel_id=1, source_target_pairs={{0,8},{1,9},{2,10},{3,11},{4,12},{5,13},{6,14},{7,15},{8,0},{9,1},... | collective-permute-start | bytes 98312 | tf_op jit(solution)/shard_map/ppermute | solution.py:254
  12.0 2.2 %collective-permute-done.2 = f32[4,16,128]{2,1,0:T(8,128)S(1)} collective-permute-done((f32[4,16,128]{2,1,0:T(8,128)S(1)}, f32[4,16,128]{2,1,0:T(8,128)S(1)}, u32[]{:S(2)}, u32[]{:S(2)}) %collective-permute-start.2) | collective-permute-done | bytes 32800 | tf_op jit(solution)/shard_map/ppermute | solution.py:254
  14.2 1.7 %collective-permute-start.3 = (f32[8,16,128]{2,1,0:T(8,128)S(1)}, f32[8,16,128]{2,1,0:T(8,128)S(1)}, u32[]{:S(2)}, u32[]{:S(2)}) collective-permute-start(f32[8,16,128]{2,1,0:T(8,128)S(1)} %pad_maximum_fusion.2), channel_id=1, source_target_pairs={{0,16},{1,17},{2,18},{3,19},{4,20},{5,21},{6,22},{7,23},{8,24},{9,... | collective-permute-start | bytes 196616 | tf_op jit(solution)/shard_map/ppermute | solution.py:254
  15.9 2.6 %collective-permute-done.3 = f32[8,16,128]{2,1,0:T(8,128)S(1)} collective-permute-done((f32[8,16,128]{2,1,0:T(8,128)S(1)}, f32[8,16,128]{2,1,0:T(8,128)S(1)}, u32[]{:S(2)}, u32[]{:S(2)}) %collective-permute-start.3) | collective-permute-done | bytes 65568 | tf_op jit(solution)/shard_map/ppermute | solution.py:254
  18.5 0.1 collective-permute-start.4
  18.6 1.3 %collective-permute-done.4 = f32[16,16,128]{2,1,0:T(8,128)S(1)} collective-permute-done((f32[16,16,128]{2,1,0:T(8,128)S(1)}, f32[16,16,128]{2,1,0:T(8,128)S(1)}, u32[]{:S(2)}, u32[]{:S(2)}) %collective-permute-start.4) | collective-permute-done | bytes 131104 | tf_op jit(solution)/shard_map/ppermute | solution.py:254
  19.9 6.6 %shard_map.39 = f32[16384,128]{1,0:T(8,128)} custom-call(s32[1]{0:T(128)} %bitcast.key_ref, f32[32,16,128]{2,1,0:T(8,128)S(1)} %pad_maximum_fusion.rec_ref, bf16[2,192,512]{2,1,0:T(8,128)(2,1)S(1)} %shard_map.37.weight_ref, bf16[2,2,256,256]{3,2,1,0:T(8,128)(2,1)S(1)} %shard_map.38.dft_ref), custom_call_target="tpu_custom_call" | custom-call | flops 10000000000 | bytes 10000000 | tf_op jit(solution)/shard_map/pallas_call | solution.py:262
  (5 shorter events, 0.0 us)
Async XLA Ops:
  0.7 5.8 %collective-permute-start = (f32[1,16,128]{2,1,0:T(8,128)S(1)}, f32[1,16,128]{2,1,0:T(8,128)S(1)}, u32[]{:S(2)}, u32[]{:S(2)}) collective-permute-start(f32[1,16,128]{2,1,0:T(8,128)S(1)} %reshape.13), channel_id=1, source_target_pairs={{0,2},{1,3},{2,0},{3,1},{4,6},{5,7},{6,4},{7,5},{8,10},{9,11},{10,... | collective-permute-start | bytes 24584 | tf_op jit(solution)/shard_map/ppermute | solution.py:254
  6.5 3.8 %collective-permute-start.1 = (f32[2,16,128]{2,1,0:T(8,128)S(1)}, f32[2,16,128]{2,1,0:T(8,128)S(1)}, u32[]{:S(2)}, u32[]{:S(2)}) collective-permute-start(f32[2,16,128]{2,1,0:T(8,128)S(1)} %pad_maximum_fusion.4), channel_id=1, source_target_pairs={{0,1},{1,0},{2,3},{3,2},{4,5},{5,4},{6,7},{7,6},{8,9},{9,8},{10,11... | collective-permute-start | bytes 49160 | tf_op jit(solution)/shard_map/ppermute | solution.py:254
  10.3 3.9 %collective-permute-start.2 = (f32[4,16,128]{2,1,0:T(8,128)S(1)}, f32[4,16,128]{2,1,0:T(8,128)S(1)}, u32[]{:S(2)}, u32[]{:S(2)}) collective-permute-start(f32[4,16,128]{2,1,0:T(8,128)S(1)} %pad_maximum_fusion.3), channel_id=1, source_target_pairs={{0,8},{1,9},{2,10},{3,11},{4,12},{5,13},{6,14},{7,15},{8,0},{9,1},... | collective-permute-start | bytes 98312 | tf_op jit(solution)/shard_map/ppermute | solution.py:254
  14.2 4.3 %collective-permute-start.3 = (f32[8,16,128]{2,1,0:T(8,128)S(1)}, f32[8,16,128]{2,1,0:T(8,128)S(1)}, u32[]{:S(2)}, u32[]{:S(2)}) collective-permute-start(f32[8,16,128]{2,1,0:T(8,128)S(1)} %pad_maximum_fusion.2), channel_id=1, source_target_pairs={{0,16},{1,17},{2,18},{3,19},{4,20},{5,21},{6,22},{7,23},{8,24},{9,... | collective-permute-start | bytes 196616 | tf_op jit(solution)/shard_map/ppermute | solution.py:254
  18.5 1.4 %collective-permute-start.4 = (f32[16,16,128]{2,1,0:T(8,128)S(1)}, f32[16,16,128]{2,1,0:T(8,128)S(1)}, u32[]{:S(2)}, u32[]{:S(2)}) collective-permute-start(f32[16,16,128]{2,1,0:T(8,128)S(1)} %pad_maximum_fusion.1), channel_id=1, source_target_pairs={{0,4},{1,5},{2,6},{3,7},{4,0},{5,1},{6,2},{7,3},{8,12},{9,13},{10,... | collective-permute-start | bytes 393224 | tf_op jit(solution)/shard_map/ppermute | solution.py:254

commit v4 on v3

--- a/solution.py
+++ b/solution.py
@@ -13,8 +13,9 @@
 P_SIZE = 256
 HOP = 64
 LANES = 128
+SUBLANES = 8
 HALF = P_SIZE // 2
-GROUP = 4
+GROUP = 2
 
 
 def split_table(table):
@@ -44,11 +45,6 @@
     return np.concatenate([upper, lower], axis=0)
 
 
-def halves(x):
-    high = x.astype(jnp.bfloat16)
-    return high, (x - high.astype(jnp.float32)).astype(jnp.bfloat16)
-
-
 def dot(a, b, contract=(1, 0)):
     return lax.dot_general(
         a,
@@ -62,7 +58,7 @@
     return sum(((index >> bit) & 1) << stage for stage, bit in enumerate(order))
 
 
-def fetch_weights(widths, offset_ref, table_ref, weight_ref, sem):
+def fetch_weights(widths, offset_ref, table_ref, weight_ref, held_ref, sem):
     copies = []
     start = 0
     for which, width in enumerate(widths):
@@ -71,7 +67,7 @@
             copies.append(
                 pltpu.make_async_copy(
                     table_ref.at[:, part, pl.ds(offset, width)],
-                    weight_ref.at[:, pl.ds(start, width)],
+                    held_ref.at[:, pl.ds(start, width)],
                     sem.at[len(copies)],
                 )
             )
@@ -80,29 +76,34 @@
         copy.start()
     for copy in copies:
         copy.wait()
-
-
-def fetch_whole(table_ref, copy_ref, sem):
-    copy = pltpu.make_async_copy(table_ref, copy_ref, sem)
+    weight_ref[...] = held_ref[...].astype(jnp.float32)
+
+
+def fetch_whole(table_ref, whole_ref, held_ref, sem):
+    copy = pltpu.make_async_copy(table_ref, held_ref, sem.at[0])
     copy.start()
     copy.wait()
-
-
-def spectra_of(window, widths, real_ref, imag_ref, weight_ref, frame_ref):
-    lower = lax.broadcasted_iota(jnp.int32, (HALF, LANES), 1) < HOP
-    for part, ref in enumerate((real_ref, imag_ref)):
-        shifts = [ref[window * HALF + i : window * HALF + i + HALF] for i in range(3)]
-        turned = [pltpu.roll(x, HOP, 1) for x in shifts]
-        odd = [jnp.where(lower, turned[i], turned[i + 1]) for i in range(2)]
-        for start, pieces in ((0, shifts[:2]), (HALF, odd)):
-            for i, piece in enumerate(pieces):
-                high, low = halves(piece)
-                column = (2 * part + i) * LANES
-                frame_ref[0, start : start + HALF, column : column + LANES] = high
-                frame_ref[1, start : start + HALF, column : column + LANES] = low
-    spectra = dot(weight_ref[0], frame_ref[0], (1, 1))
-    spectra += dot(weight_ref[0], frame_ref[1], (1, 1))
-    spectra += dot(weight_ref[1], frame_ref[0], (1, 1))
+    whole_ref[...] = held_ref[...].astype(jnp.float32)
+
+
+def rounded_off(x):
+    return x - x.astype(jnp.bfloat16).astype(jnp.float32)
+
+
+def spectra_of(window, widths, sample_ref, weight_ref):
+    def frames(low):
+        return jnp.concatenate([
+            jnp.concatenate([
+                sample_ref[part, odd, low, window * HALF + i : window * HALF + i + HALF]
+                for part in range(2)
+                for i in range(2)
+            ], axis=1)
+            for odd in range(2)
+        ])
+    count = 2 * sum(widths)
+    both = dot(weight_ref[...].reshape(2 * count, 2 * C), frames(0), (1, 1))
+    spectra = both[:count] + both[count:]
+    spectra += dot(weight_ref[0], frames(1), (1, 1))
     found = []
     start = 0
     for width in widths:
@@ -125,7 +126,7 @@
 
 
 def kernel(order, sizes, key_ref, rec_ref, weight_ref, dft_ref, out_ref,
-           real_ref, imag_ref, frame_ref, first_ref, second_ref, even_ref, odd_ref, total_ref, sem):
+           sample_ref, first_ref, second_ref, even_ref, odd_ref, total_ref, sem):
     devices, widths, windows = sizes
     lead_width, trail_width = widths
     block = rec_ref.shape[1] // 2
@@ -136,15 +137,23 @@
 
     key = key_ref[0]
     for device in range(devices):
-        slot = key ^ slot_of(device, order)
-        piece = rec_ref[slot]
-        real_ref[device * block : (device + 1) * block] = piece[:block]
-        imag_ref[device * block : (device + 1) * block] = piece[block:]
-    zeros = jnp.zeros((8, LANES), jnp.float32)
-    real_ref[rows : rows + 8] = zeros
-    imag_ref[rows : rows + 8] = zeros
+        piece = rec_ref[key ^ slot_of(device, order)]
+        for part in range(2):
+            place = slice(device * block, (device + 1) * block)
+            sample_ref[part, 0, 0, place] = piece[part * block : (part + 1) * block]
+    lower = lax.broadcasted_iota(jnp.int32, (rows, LANES), 1) < HOP
+    zeros = jnp.zeros((SUBLANES, LANES), jnp.float32)
+    for part in range(2):
+        sample_ref[part, 0, 0, rows:] = zeros
+        turned = [
+            pltpu.roll(sample_ref[part, 0, 0, i : i + rows], HOP, 1) for i in range(2)
+        ]
+        sample_ref[part, 1, 0, :rows] = jnp.where(lower, turned[0], turned[1])
+        sample_ref[part, 1, 0, rows:] = zeros
+        for odd in range(2):
+            sample_ref[part, odd, 1] = rounded_off(sample_ref[part, odd, 0])
     for window in range(windows):
-        lead, trail = spectra_of(window, widths, real_ref, imag_ref, weight_ref, frame_ref)
+        lead, trail = spectra_of(window, widths, sample_ref, weight_ref)
         for i in range(4):
             second_ref[i, pl.ds(window, trail_width, stride=windows), :] = trail[i]
             for copy in range(pattern // windows):
@@ -162,10 +171,9 @@
                     ar, ai = lead[2 * odd : 2 * odd + 2]
                     br, bi = trail[2 * odd : 2 * odd + 2]
                     for part, value in enumerate((ar * br + ai * bi, ai * br - ar * bi)):
-                        high, low = halves(value)
                         column = part * LANES
-                        z_ref[odd, 0, row : row + pattern, column : column + LANES] = high
-                        z_ref[odd, 1, row : row + pattern, column : column + LANES] = low
+                        z_ref[odd, 0, row : row + pattern, column : column + LANES] = value
+                        z_ref[odd, 1, row : row + pattern, column : column + LANES] = rounded_off(value)
 
     def copy_out(step):
         size = GROUP * height * 4
@@ -191,27 +199,26 @@
                     ]
         copy_out(step).start()
 
+    refs = (even_ref, odd_ref)
     multiply(0, even_ref)
 
-    @pl.loop(0, steps, step=2)
-    def _(step):
-        multiply(step + 1, odd_ref)
-        transform(step, even_ref)
-        multiply(jnp.minimum(step + 2, steps - 1), even_ref)
-        transform(step + 1, odd_ref)
+    for step in range(steps):
+        if step + 1 < steps:
+            multiply(step + 1, refs[(step + 1) % 2])
+        transform(step, refs[step % 2])
 
     for step in range(steps):
         copy_out(step).wait()
 
 
-def fetched(body, scalars, table, shape, sem):
+def fetched(body, scalars, table, shape):
     return pl.pallas_call(
         body,
-        out_shape=jax.ShapeDtypeStruct(shape, table.dtype),
+        out_shape=jax.ShapeDtypeStruct(shape, jnp.float32),
         in_specs=[pl.BlockSpec(memory_space=pltpu.SMEM)] * len(scalars)
         + [pl.BlockSpec(memory_space=pltpu.HBM)],
         out_specs=pl.BlockSpec(memory_space=pltpu.VMEM),
-        scratch_shapes=[sem],
+        scratch_shapes=[pltpu.VMEM(shape, jnp.bfloat16), pltpu.SemaphoreType.DMA((4,))],
         compiler_params=pltpu.CompilerParams(vmem_limit_bytes=8 * 2**20),
         cost_estimate=pl.CostEstimate(flops=10**9, bytes_accessed=10**6, transcendentals=0),
     )(*scalars, pltpu.with_memory_space_constraint(jnp.asarray(table), pltpu.HBM))
@@ -240,16 +247,15 @@
         (offsets,),
         np.stack(split_table(channel_table())),
         (2, 2 * sum(widths), 2 * C),
-        pltpu.SemaphoreType.DMA((4,)),
     )
     dft = np.stack([np.stack(split_table(window_table(odd))) for odd in range(2)])
-    dft = fetched(fetch_whole, (), dft, dft.shape, pltpu.SemaphoreType.DMA(()))
+    dft = fetched(fetch_whole, (), dft, dft.shape)
     blocks = record.reshape(1, 2 * samples // LANES, LANES)
     for stage, bit in enumerate(order):
         if stage == 1:
+            blocks, dft = lax.optimization_barrier((blocks, dft))
+        if stage == 2:
             blocks, weights = lax.optimization_barrier((blocks, weights))
-        if stage == 2:
-            blocks, dft = lax.optimization_barrier((blocks, dft))
         route = [(i, i ^ (1 << bit)) for i in range(devices)]
         blocks = jnp.concatenate([blocks, lax.ppermute(blocks, axes, route)], axis=0)
 
@@ -265,13 +271,11 @@
         in_specs=[smem, vmem, vmem, vmem],
         out_specs=pl.BlockSpec(memory_space=pltpu.HBM),
         scratch_shapes=[
-            pltpu.VMEM((devices * samples // LANES + 8, LANES), jnp.float32),
-            pltpu.VMEM((devices * samples // LANES + 8, LANES), jnp.float32),
-            pltpu.VMEM((2, P_SIZE, 2 * C), jnp.bfloat16),
+            pltpu.VMEM((2, 2, 2, devices * samples // LANES + SUBLANES, LANES), jnp.float32),
             pltpu.VMEM((4, lead_width * pattern, LANES), jnp.float32),
             pltpu.VMEM((4, height, LANES), jnp.float32),
-            pltpu.VMEM((2, 2, GROUP * height, 2 * LANES), jnp.bfloat16),
-            pltpu.VMEM((2, 2, GROUP * height, 2 * LANES), jnp.bfloat16),
+            pltpu.VMEM((2, 2, GROUP * height, 2 * LANES), jnp.float32),
+            pltpu.VMEM((2, 2, GROUP * height, 2 * LANES), jnp.float32),
             pltpu.VMEM((lead_width * height * 4, LANES), jnp.float32),
             pltpu.SemaphoreType.DMA((lead_width // GROUP,)),
         ],

time: 26.8 us -> 25.7 us (0.959)
  Pallas kernels: 9.3 us -> 8.47 us
  waiting for transfers between devices: 7.07 us -> 6.37 us
  starting transfers between devices: 9.32 us -> 9.72 us
    pallas_call x1, Pallas kernels: 6.63 us -> 5.66 us  [local(): pl.pallas_call(functools.partial(kernel, order, sizes), out_shape=jax.Sha...]
    ppermute x5, waiting for transfers between devices: 7.07 us -> 6.37 us  [local(): lax.ppermute(blocks, axes, route)]
    ppermute x5, starting transfers between devices: 9.32 us -> 9.72 us  [local(): lax.ppermute(blocks, axes, route)]
  transfers between devices with their start and end apart: 5 -> 5, of which waited for: 4 -> 5; matrix products, arithmetic and copies ran while one was open for 0% -> 0% of each run, Pallas kernels for 10% -> 11%
where the time goes in v4:
time: 25.7 us; the launch traced here: 25.4 us
  starting transfers between devices  9.72 us (38%)
  Pallas kernels  8.47 us (33%)
  waiting for transfers between devices  6.37 us (25%)
  local copies, waits for them, and re-layouts  0.71 us (3%)
    ppermute x5, starting transfers between devices, local(): lax.ppermute(blocks, axes, route)  9.72 us
    ppermute x5, waiting for transfers between devices, local(): lax.ppermute(blocks, axes, route)  6.37 us
    pallas_call x1, Pallas kernels, local(): pl.pallas_call(functools.partial(kernel, order, sizes), out_shape=jax.Sha...  5.66 us
    pallas_call x2, Pallas kernels, fetched(): pl.pallas_call(body, out_shape=jax.ShapeDtypeStruct(shape, jnp.float32),...  2.81 us
    reshape x1, local copies, waits for them, and re-layouts, local(): blocks = record.reshape(1, 2 * samples // LANES, LANES)  0.71 us
  transfers between devices with their start and end apart: 5, of which 5 were waited for; matrix products, arithmetic and copies ran while one was open for 0% of the time, Pallas kernels for 11%

profile of v4, /device:TPU:0, one launch (start us, length us, event | category | flops | bytes accessed | tf_op | source)
XLA Modules:
  0.0 25.4 jit_solution(16968821604169529013)
XLA Ops:
  0.0 0.7 %reshape.13 = f32[1,16,128]{2,1,0:T(8,128)S(1)} reshape(f32[2,1024]{1,0:T(2,128)} %param.3) | data formatting | bytes 16384 | tf_op jit(solution)/shard_map/reshape | solution.py:253
  0.7 4.1 %collective-permute-start = (f32[1,16,128]{2,1,0:T(8,128)S(1)}, f32[1,16,128]{2,1,0:T(8,128)S(1)}, u32[]{:S(2)}, u32[]{:S(2)}) collective-permute-start(f32[1,16,128]{2,1,0:T(8,128)S(1)} %reshape.13), channel_id=1, source_target_pairs={{0,2},{1,3},{2,0},{3,1},{4,6},{5,7},{6,4},{7,5},{8,10},{9,11},{10,... | collective-permute-start | bytes 24584 | tf_op jit(solution)/shard_map/ppermute | solution.py:260
  4.8 0.1 pad_add_fusion.offset_ref
  4.8 1.1 %shard_map.37.dft_ref = f32[2,2,256,256]{3,2,1,0:T(8,128)S(1)} custom-call(bf16[2,2,256,256]{3,2,1,0:T(8,128)(2,1)} %constant.28.clone.table_ref), custom_call_target="tpu_custom_call" | custom-call | flops 1000000000 | bytes 1000000 | tf_op jit(solution)/shard_map/pallas_call | solution.py:215
  6.0 0.4 %collective-permute-done = f32[1,16,128]{2,1,0:T(8,128)S(1)} collective-permute-done((f32[1,16,128]{2,1,0:T(8,128)S(1)}, f32[1,16,128]{2,1,0:T(8,128)S(1)}, u32[]{:S(2)}, u32[]{:S(2)}) %collective-permute-start) | collective-permute-done | bytes 8224 | tf_op jit(solution)/shard_map/ppermute | solution.py:260
  6.4 1.9 %collective-permute-start.1 = (f32[2,16,128]{2,1,0:T(8,128)S(1)}, f32[2,16,128]{2,1,0:T(8,128)S(1)}, u32[]{:S(2)}, u32[]{:S(2)}) collective-permute-start(f32[2,16,128]{2,1,0:T(8,128)S(1)} %pad_maximum_fusion.4), channel_id=1, source_target_pairs={{0,1},{1,0},{2,3},{3,2},{4,5},{5,4},{6,7},{7,6},{8,9},{9,8},{10,11... | collective-permute-start | bytes 49160 | tf_op jit(solution)/shard_map/ppermute | solution.py:260
  8.3 1.7 %shard_map.38.weight_ref = f32[2,192,512]{2,1,0:T(8,128)S(1)} custom-call(s32[2]{0:T(128)S(1)} %pad_add_fusion.offset_ref, bf16[2,2,256,512]{3,2,1,0:T(8,128)(2,1)} %constant.27.clone.table_ref), custom_call_target="tpu_custom_call" | custom-call | flops 1000000000 | bytes 1000000 | tf_op jit(solution)/shard_map/pallas_call | solution.py:215
  10.0 0.2 collective-permute-done.1
  10.1 1.8 %collective-permute-start.2 = (f32[4,16,128]{2,1,0:T(8,128)S(1)}, f32[4,16,128]{2,1,0:T(8,128)S(1)}, u32[]{:S(2)}, u32[]{:S(2)}) collective-permute-start(f32[4,16,128]{2,1,0:T(8,128)S(1)} %pad_maximum_fusion.3), channel_id=1, source_target_pairs={{0,8},{1,9},{2,10},{3,11},{4,12},{5,13},{6,14},{7,15},{8,0},{9,1},... | collective-permute-start | bytes 98312 | tf_op jit(solution)/shard_map/ppermute | solution.py:260
  12.0 2.1 %collective-permute-done.2 = f32[4,16,128]{2,1,0:T(8,128)S(1)} collective-permute-done((f32[4,16,128]{2,1,0:T(8,128)S(1)}, f32[4,16,128]{2,1,0:T(8,128)S(1)}, u32[]{:S(2)}, u32[]{:S(2)}) %collective-permute-start.2) | collective-permute-done | bytes 32800 | tf_op jit(solution)/shard_map/ppermute | solution.py:260
  14.1 1.9 %collective-permute-start.3 = (f32[8,16,128]{2,1,0:T(8,128)S(1)}, f32[8,16,128]{2,1,0:T(8,128)S(1)}, u32[]{:S(2)}, u32[]{:S(2)}) collective-permute-start(f32[8,16,128]{2,1,0:T(8,128)S(1)} %pad_maximum_fusion.2), channel_id=1, source_target_pairs={{0,16},{1,17},{2,18},{3,19},{4,20},{5,21},{6,22},{7,23},{8,24},{9,... | collective-permute-start | bytes 196616 | tf_op jit(solution)/shard_map/ppermute | solution.py:260
  15.9 2.4 %collective-permute-done.3 = f32[8,16,128]{2,1,0:T(8,128)S(1)} collective-permute-done((f32[8,16,128]{2,1,0:T(8,128)S(1)}, f32[8,16,128]{2,1,0:T(8,128)S(1)}, u32[]{:S(2)}, u32[]{:S(2)}) %collective-permute-start.3) | collective-permute-done | bytes 65568 | tf_op jit(solution)/shard_map/ppermute | solution.py:260
  18.3 0.1 collective-permute-start.4
  18.4 1.3 %collective-permute-done.4 = f32[16,16,128]{2,1,0:T(8,128)S(1)} collective-permute-done((f32[16,16,128]{2,1,0:T(8,128)S(1)}, f32[16,16,128]{2,1,0:T(8,128)S(1)}, u32[]{:S(2)}, u32[]{:S(2)}) %collective-permute-start.4) | collective-permute-done | bytes 131104 | tf_op jit(solution)/shard_map/ppermute | solution.py:260
  19.8 5.7 %shard_map.39 = f32[16384,128]{1,0:T(8,128)} custom-call(s32[1]{0:T(128)} %bitcast.key_ref, f32[32,16,128]{2,1,0:T(8,128)S(1)} %pad_maximum_fusion.rec_ref, f32[2,192,512]{2,1,0:T(8,128)S(1)} %shard_map.38.weight_ref, f32[2,2,256,256]{3,2,1,0:T(8,128)S(1)} %shard_map.37.dft_ref), custom_call_target="tpu_custom_call" | custom-call | flops 10000000000 | bytes 10000000 | tf_op jit(solution)/shard_map/pallas_call | solution.py:268
  (5 shorter events, 0.0 us)
Async XLA Ops:
  0.7 5.7 %collective-permute-start = (f32[1,16,128]{2,1,0:T(8,128)S(1)}, f32[1,16,128]{2,1,0:T(8,128)S(1)}, u32[]{:S(2)}, u32[]{:S(2)}) collective-permute-start(f32[1,16,128]{2,1,0:T(8,128)S(1)} %reshape.13), channel_id=1, source_target_pairs={{0,2},{1,3},{2,0},{3,1},{4,6},{5,7},{6,4},{7,5},{8,10},{9,11},{10,... | collective-permute-start | bytes 24584 | tf_op jit(solution)/shard_map/ppermute | solution.py:260
  6.4 3.7 %collective-permute-start.1 = (f32[2,16,128]{2,1,0:T(8,128)S(1)}, f32[2,16,128]{2,1,0:T(8,128)S(1)}, u32[]{:S(2)}, u32[]{:S(2)}) collective-permute-start(f32[2,16,128]{2,1,0:T(8,128)S(1)} %pad_maximum_fusion.4), channel_id=1, source_target_pairs={{0,1},{1,0},{2,3},{3,2},{4,5},{5,4},{6,7},{7,6},{8,9},{9,8},{10,11... | collective-permute-start | bytes 49160 | tf_op jit(solution)/shard_map/ppermute | solution.py:260
  10.1 3.9 %collective-permute-start.2 = (f32[4,16,128]{2,1,0:T(8,128)S(1)}, f32[4,16,128]{2,1,0:T(8,128)S(1)}, u32[]{:S(2)}, u32[]{:S(2)}) collective-permute-start(f32[4,16,128]{2,1,0:T(8,128)S(1)} %pad_maximum_fusion.3), channel_id=1, source_target_pairs={{0,8},{1,9},{2,10},{3,11},{4,12},{5,13},{6,14},{7,15},{8,0},{9,1},... | collective-permute-start | bytes 98312 | tf_op jit(solution)/shard_map/ppermute | solution.py:260
  14.1 4.3 %collective-permute-start.3 = (f32[8,16,128]{2,1,0:T(8,128)S(1)}, f32[8,16,128]{2,1,0:T(8,128)S(1)}, u32[]{:S(2)}, u32[]{:S(2)}) collective-permute-start(f32[8,16,128]{2,1,0:T(8,128)S(1)} %pad_maximum_fusion.2), channel_id=1, source_target_pairs={{0,16},{1,17},{2,18},{3,19},{4,20},{5,21},{6,22},{7,23},{8,24},{9,... | collective-permute-start | bytes 196616 | tf_op jit(solution)/shard_map/ppermute | solution.py:260
  18.3 1.4 %collective-permute-start.4 = (f32[16,16,128]{2,1,0:T(8,128)S(1)}, f32[16,16,128]{2,1,0:T(8,128)S(1)}, u32[]{:S(2)}, u32[]{:S(2)}) collective-permute-start(f32[16,16,128]{2,1,0:T(8,128)S(1)} %pad_maximum_fusion.1), channel_id=1, source_target_pairs={{0,4},{1,5},{2,6},{3,7},{4,0},{5,1},{6,2},{7,3},{8,12},{9,13},{10,... | collective-permute-start | bytes 393224 | tf_op jit(solution)/shard_map/ppermute | solution.py:260

commit v5 on v4

--- a/solution.py
+++ b/solution.py
@@ -79,10 +79,15 @@
     weight_ref[...] = held_ref[...].astype(jnp.float32)
 
 
-def fetch_whole(table_ref, whole_ref, held_ref, sem):
-    copy = pltpu.make_async_copy(table_ref, held_ref, sem.at[0])
-    copy.start()
-    copy.wait()
+def fetch_whole(own_ref, table_ref, own_copy_ref, whole_ref, held_ref, sem):
+    copies = [
+        pltpu.make_async_copy(own_ref, own_copy_ref, sem.at[0]),
+        pltpu.make_async_copy(table_ref, held_ref, sem.at[1]),
+    ]
+    for copy in copies:
+        copy.start()
+    for copy in copies:
+        copy.wait()
     whole_ref[...] = held_ref[...].astype(jnp.float32)
 
 
@@ -137,10 +142,10 @@
 
     key = key_ref[0]
     for device in range(devices):
-        piece = rec_ref[key ^ slot_of(device, order)]
+        slot = key ^ slot_of(device, order)
         for part in range(2):
             place = slice(device * block, (device + 1) * block)
-            sample_ref[part, 0, 0, place] = piece[part * block : (part + 1) * block]
+            sample_ref[part, 0, 0, place] = rec_ref[slot, pl.ds(part, block, stride=2), :]
     lower = lax.broadcasted_iota(jnp.int32, (rows, LANES), 1) < HOP
     zeros = jnp.zeros((SUBLANES, LANES), jnp.float32)
     for part in range(2):
@@ -187,8 +192,8 @@
             for odd in range(2):
                 high = z_ref[odd, 0, row : row + chunk]
                 low = z_ref[odd, 1, row : row + chunk]
-                total = dot(high, dft_ref[odd, 0])
-                total += dot(low, dft_ref[odd, 0])
+                total = dot(low, dft_ref[odd, 0])
+                total += dot(high, dft_ref[odd, 0])
                 total += dot(high, dft_ref[odd, 1])
                 sums.append(total)
             base = pl.multiple_of((step * GROUP * height + row) * 4, 4 * chunk)
@@ -211,17 +216,19 @@
         copy_out(step).wait()
 
 
-def fetched(body, scalars, table, shape):
+def fetched(body, scalars, arrays, shapes, table):
+    vmem = pl.BlockSpec(memory_space=pltpu.VMEM)
+    in_hbm = [pltpu.with_memory_space_constraint(x, pltpu.HBM) for x in (*arrays, jnp.asarray(table))]
     return pl.pallas_call(
         body,
-        out_shape=jax.ShapeDtypeStruct(shape, jnp.float32),
+        out_shape=[jax.ShapeDtypeStruct(shape, jnp.float32) for shape in shapes],
         in_specs=[pl.BlockSpec(memory_space=pltpu.SMEM)] * len(scalars)
-        + [pl.BlockSpec(memory_space=pltpu.HBM)],
-        out_specs=pl.BlockSpec(memory_space=pltpu.VMEM),
-        scratch_shapes=[pltpu.VMEM(shape, jnp.bfloat16), pltpu.SemaphoreType.DMA((4,))],
+        + [pl.BlockSpec(memory_space=pltpu.HBM)] * len(in_hbm),
+        out_specs=[vmem] * len(shapes),
+        scratch_shapes=[pltpu.VMEM(shapes[-1], jnp.bfloat16), pltpu.SemaphoreType.DMA((4,))],
         compiler_params=pltpu.CompilerParams(vmem_limit_bytes=8 * 2**20),
         cost_estimate=pl.CostEstimate(flops=10**9, bytes_accessed=10**6, transcendentals=0),
-    )(*scalars, pltpu.with_memory_space_constraint(jnp.asarray(table), pltpu.HBM))
+    )(*scalars, *in_hbm)
 
 
 def local(record):
@@ -242,22 +249,25 @@
     order = tuple(col_bits[::-1] + row_bits[1:] + row_bits[:1])
     widths = (lead_width, trail_width)
     offsets = jnp.stack([row_index * lead_width, col_index * trail_width]).astype(jnp.int32)
-    weights = fetched(
+    [weights] = fetched(
         functools.partial(fetch_weights, widths),
         (offsets,),
+        (),
+        [(2, 2 * sum(widths), 2 * C)],
         np.stack(split_table(channel_table())),
-        (2, 2 * sum(widths), 2 * C),
     )
+    own = record.reshape(2, samples // LANES, LANES).transpose(1, 0, 2)
+    own = own.reshape(1, 2 * samples // LANES, LANES)
     dft = np.stack([np.stack(split_table(window_table(odd))) for odd in range(2)])
-    dft = fetched(fetch_whole, (), dft, dft.shape)
-    blocks = record.reshape(1, 2 * samples // LANES, LANES)
+    blocks, dft = fetched(fetch_whole, (), (own,), [own.shape, dft.shape], dft)
     for stage, bit in enumerate(order):
+        route = [(i, i ^ (1 << bit)) for i in range(devices)]
+        received = lax.ppermute(blocks if stage else own, axes, route)
+        blocks = jnp.concatenate([blocks, received], axis=0)
+        if stage == 0:
+            blocks, dft = lax.optimization_barrier((blocks, dft))
         if stage == 1:
-            blocks, dft = lax.optimization_barrier((blocks, dft))
-        if stage == 2:
             blocks, weights = lax.optimization_barrier((blocks, weights))
-        route = [(i, i ^ (1 << bit)) for i in range(devices)]
-        blocks = jnp.concatenate([blocks, lax.ppermute(blocks, axes, route)], axis=0)
 
     key = slot_of(me, order).astype(jnp.int32).reshape(1)
     height = trail_width * windows

time: 25.7 us -> 25 us (0.973)
  local copies, waits for them, and re-layouts: 0.71 us -> 0 us
    reshape x1 -> x0, local copies, waits for them, and re-layouts: 0.71 us -> none  [local(): blocks = record.reshape(1, 2 * samples // LANES, LANES)]
where the time goes in v5:
time: 25 us; the launch traced here: 24.8 us
  starting transfers between devices  9.72 us (39%)
  Pallas kernels  8.3 us (33%)
  waiting for transfers between devices  6.57 us (26%)
    ppermute x5, starting transfers between devices, local(): received = lax.ppermute(blocks if stage else own, axes, route)  9.72 us
    ppermute x5, waiting for transfers between devices, local(): received = lax.ppermute(blocks if stage else own, axes, route)  6.57 us
    pallas_call x1, Pallas kernels, local(): pl.pallas_call(functools.partial(kernel, order, sizes), out_shape=jax.Sha...  5.48 us
    pallas_call x2, Pallas kernels, fetched(): pl.pallas_call(body, out_shape=[jax.ShapeDtypeStruct(shape, jnp.float32)...  2.83 us
  transfers between devices with their start and end apart: 5, of which 5 were waited for; matrix products, arithmetic and copies ran while one was open for 0% of the time, Pallas kernels for 11%

profile of v5, /device:TPU:0, one launch (start us, length us, event | category | flops | bytes accessed | tf_op | source)
XLA Modules:
  0.0 24.8 jit_solution(9459998310128315435)
XLA Ops:
  0.0 4.1 %collective-permute-start = (f32[1,16,128]{2,1,0:T(8,128)}, f32[1,16,128]{2,1,0:T(8,128)S(1)}, u32[]{:S(2)}, u32[]{:S(2)}) collective-permute-start(f32[1,16,128]{2,1,0:T(8,128)} %bitcast.13), channel_id=1, source_target_pairs={{0,2},{1,3},{2,0},{3,1},{4,6},{5,7},{6,4},{7,5},{8,10},{9,11},{10,... | collective-permute-start | bytes 24584 | tf_op jit(solution)/shard_map/ppermute | solution.py:265
  4.1 0.1 pad_add_fusion.offset_ref
  4.1 1.2 %shard_map.37 = (f32[1,16,128]{2,1,0:T(8,128)S(1)}, f32[2,2,256,256]{3,2,1,0:T(8,128)S(1)}) custom-call(f32[1,16,128]{2,1,0:T(8,128)} %bitcast.14, bf16[2,2,256,256]{3,2,1,0:T(8,128)(2,1)} %constant.28.clone.table_ref), custom_call_target="tpu_custom_call" | custom-call | flops 1000000000 | bytes 1000000 | tf_op jit(solution)/shard_map/pallas_call | solution.py:222
  5.3 0.6 %collective-permute-done = f32[1,16,128]{2,1,0:T(8,128)S(1)} collective-permute-done((f32[1,16,128]{2,1,0:T(8,128)}, f32[1,16,128]{2,1,0:T(8,128)S(1)}, u32[]{:S(2)}, u32[]{:S(2)}) %collective-permute-start) | collective-permute-done | bytes 8224 | tf_op jit(solution)/shard_map/ppermute | solution.py:265
  5.9 1.9 %collective-permute-start.1 = (f32[2,16,128]{2,1,0:T(8,128)S(1)}, f32[2,16,128]{2,1,0:T(8,128)S(1)}, u32[]{:S(2)}, u32[]{:S(2)}) collective-permute-start(f32[2,16,128]{2,1,0:T(8,128)S(1)} %pad_maximum_fusion.4), channel_id=1, source_target_pairs={{0,1},{1,0},{2,3},{3,2},{4,5},{5,4},{6,7},{7,6},{8,9},{9,8},{10,11... | collective-permute-start | bytes 49160 | tf_op jit(solution)/shard_map/ppermute | solution.py:265
  7.8 1.7 %shard_map.38.weight_ref = f32[2,192,512]{2,1,0:T(8,128)S(1)} custom-call(s32[2]{0:T(128)S(1)} %pad_add_fusion.offset_ref, bf16[2,2,256,512]{3,2,1,0:T(8,128)(2,1)} %constant.27.clone.table_ref), custom_call_target="tpu_custom_call" | custom-call | flops 1000000000 | bytes 1000000 | tf_op jit(solution)/shard_map/pallas_call | solution.py:222
  9.5 0.2 collective-permute-done.1
  9.7 1.8 %collective-permute-start.2 = (f32[4,16,128]{2,1,0:T(8,128)S(1)}, f32[4,16,128]{2,1,0:T(8,128)S(1)}, u32[]{:S(2)}, u32[]{:S(2)}) collective-permute-start(f32[4,16,128]{2,1,0:T(8,128)S(1)} %pad_maximum_fusion.3), channel_id=1, source_target_pairs={{0,8},{1,9},{2,10},{3,11},{4,12},{5,13},{6,14},{7,15},{8,0},{9,1},... | collective-permute-start | bytes 98312 | tf_op jit(solution)/shard_map/ppermute | solution.py:265
  11.5 2.1 %collective-permute-done.2 = f32[4,16,128]{2,1,0:T(8,128)S(1)} collective-permute-done((f32[4,16,128]{2,1,0:T(8,128)S(1)}, f32[4,16,128]{2,1,0:T(8,128)S(1)}, u32[]{:S(2)}, u32[]{:S(2)}) %collective-permute-start.2) | collective-permute-done | bytes 32800 | tf_op jit(solution)/shard_map/ppermute | solution.py:265
  13.6 1.9 %collective-permute-start.3 = (f32[8,16,128]{2,1,0:T(8,128)S(1)}, f32[8,16,128]{2,1,0:T(8,128)S(1)}, u32[]{:S(2)}, u32[]{:S(2)}) collective-permute-start(f32[8,16,128]{2,1,0:T(8,128)S(1)} %pad_maximum_fusion.2), channel_id=1, source_target_pairs={{0,16},{1,17},{2,18},{3,19},{4,20},{5,21},{6,22},{7,23},{8,24},{9,... | collective-permute-start | bytes 196616 | tf_op jit(solution)/shard_map/ppermute | solution.py:265
  15.4 2.4 %collective-permute-done.3 = f32[8,16,128]{2,1,0:T(8,128)S(1)} collective-permute-done((f32[8,16,128]{2,1,0:T(8,128)S(1)}, f32[8,16,128]{2,1,0:T(8,128)S(1)}, u32[]{:S(2)}, u32[]{:S(2)}) %collective-permute-start.3) | collective-permute-done | bytes 65568 | tf_op jit(solution)/shard_map/ppermute | solution.py:265
  17.9 0.1 collective-permute-start.4
  17.9 1.3 %collective-permute-done.4 = f32[16,16,128]{2,1,0:T(8,128)S(1)} collective-permute-done((f32[16,16,128]{2,1,0:T(8,128)S(1)}, f32[16,16,128]{2,1,0:T(8,128)S(1)}, u32[]{:S(2)}, u32[]{:S(2)}) %collective-permute-start.4) | collective-permute-done | bytes 131104 | tf_op jit(solution)/shard_map/ppermute | solution.py:265
  19.3 5.5 %shard_map.39 = f32[16384,128]{1,0:T(8,128)} custom-call(s32[1]{0:T(128)} %bitcast.key_ref, f32[32,16,128]{2,1,0:T(8,128)S(1)} %pad_maximum_fusion.rec_ref, f32[2,192,512]{2,1,0:T(8,128)S(1)} %shard_map.38.weight_ref, f32[2,2,256,256]{3,2,1,0:T(8,128)S(1)} %get-tuple-element.16.dft_ref), custom_call_target="tpu_custom_call" | custom-call | flops 10000000000 | bytes 10000000 | tf_op jit(solution)/shard_map/pallas_call | solution.py:278
  (5 shorter events, 0.0 us)
Async XLA Ops:
  0.0 5.9 %collective-permute-start = (f32[1,16,128]{2,1,0:T(8,128)}, f32[1,16,128]{2,1,0:T(8,128)S(1)}, u32[]{:S(2)}, u32[]{:S(2)}) collective-permute-start(f32[1,16,128]{2,1,0:T(8,128)} %bitcast.13), channel_id=1, source_target_pairs={{0,2},{1,3},{2,0},{3,1},{4,6},{5,7},{6,4},{7,5},{8,10},{9,11},{10,... | collective-permute-start | bytes 24584 | tf_op jit(solution)/shard_map/ppermute | solution.py:265
  5.9 3.7 %collective-permute-start.1 = (f32[2,16,128]{2,1,0:T(8,128)S(1)}, f32[2,16,128]{2,1,0:T(8,128)S(1)}, u32[]{:S(2)}, u32[]{:S(2)}) collective-permute-start(f32[2,16,128]{2,1,0:T(8,128)S(1)} %pad_maximum_fusion.4), channel_id=1, source_target_pairs={{0,1},{1,0},{2,3},{3,2},{4,5},{5,4},{6,7},{7,6},{8,9},{9,8},{10,11... | collective-permute-start | bytes 49160 | tf_op jit(solution)/shard_map/ppermute | solution.py:265
  9.7 3.9 %collective-permute-start.2 = (f32[4,16,128]{2,1,0:T(8,128)S(1)}, f32[4,16,128]{2,1,0:T(8,128)S(1)}, u32[]{:S(2)}, u32[]{:S(2)}) collective-permute-start(f32[4,16,128]{2,1,0:T(8,128)S(1)} %pad_maximum_fusion.3), channel_id=1, source_target_pairs={{0,8},{1,9},{2,10},{3,11},{4,12},{5,13},{6,14},{7,15},{8,0},{9,1},... | collective-permute-start | bytes 98312 | tf_op jit(solution)/shard_map/ppermute | solution.py:265
  13.6 4.3 %collective-permute-start.3 = (f32[8,16,128]{2,1,0:T(8,128)S(1)}, f32[8,16,128]{2,1,0:T(8,128)S(1)}, u32[]{:S(2)}, u32[]{:S(2)}) collective-permute-start(f32[8,16,128]{2,1,0:T(8,128)S(1)} %pad_maximum_fusion.2), channel_id=1, source_target_pairs={{0,16},{1,17},{2,18},{3,19},{4,20},{5,21},{6,22},{7,23},{8,24},{9,... | collective-permute-start | bytes 196616 | tf_op jit(solution)/shard_map/ppermute | solution.py:265
  17.9 1.4 %collective-permute-start.4 = (f32[16,16,128]{2,1,0:T(8,128)S(1)}, f32[16,16,128]{2,1,0:T(8,128)S(1)}, u32[]{:S(2)}, u32[]{:S(2)}) collective-permute-start(f32[16,16,128]{2,1,0:T(8,128)S(1)} %pad_maximum_fusion.1), channel_id=1, source_target_pairs={{0,4},{1,5},{2,6},{3,7},{4,0},{5,1},{6,2},{7,3},{8,12},{9,13},{10,... | collective-permute-start | bytes 393224 | tf_op jit(solution)/shard_map/ppermute | solution.py:265

commit v6 on v5

--- a/solution.py
+++ b/solution.py
@@ -208,9 +208,9 @@
     multiply(0, even_ref)
 
     for step in range(steps):
+        transform(step, refs[step % 2])
         if step + 1 < steps:
             multiply(step + 1, refs[(step + 1) % 2])
-        transform(step, refs[step % 2])
 
     for step in range(steps):
         copy_out(step).wait()

time: 25 us -> 25 us (level)
  no operation moved by 1% of the time
where the time goes in v6:
time: 25 us; the launch traced here: 24.8 us
  starting transfers between devices  9.72 us (39%)
  Pallas kernels  8.3 us (33%)
  waiting for transfers between devices  6.57 us (26%)
    ppermute x5, starting transfers between devices, local(): received = lax.ppermute(blocks if stage else own, axes, route)  9.72 us
    ppermute x5, waiting for transfers between devices, local(): received = lax.ppermute(blocks if stage else own, axes, route)  6.57 us
    pallas_call x1, Pallas kernels, local(): pl.pallas_call(functools.partial(kernel, order, sizes), out_shape=jax.Sha...  5.48 us
    pallas_call x2, Pallas kernels, fetched(): pl.pallas_call(body, out_shape=[jax.ShapeDtypeStruct(shape, jnp.float32)...  2.83 us
  transfers between devices with their start and end apart: 5, of which 5 were waited for; matrix products, arithmetic and copies ran while one was open for 0% of the time, Pallas kernels for 11%

profile of v6, /device:TPU:0, one launch (start us, length us, event | category | flops | bytes accessed | tf_op | source)
XLA Modules:
  0.0 24.8 jit_solution(9459998310128315435)
XLA Ops:
  0.0 4.1 %collective-permute-start = (f32[1,16,128]{2,1,0:T(8,128)}, f32[1,16,128]{2,1,0:T(8,128)S(1)}, u32[]{:S(2)}, u32[]{:S(2)}) collective-permute-start(f32[1,16,128]{2,1,0:T(8,128)} %bitcast.13), channel_id=1, source_target_pairs={{0,2},{1,3},{2,0},{3,1},{4,6},{5,7},{6,4},{7,5},{8,10},{9,11},{10,... | collective-permute-start | bytes 24584 | tf_op jit(solution)/shard_map/ppermute | solution.py:265
  4.1 0.1 pad_add_fusion.offset_ref
  4.1 1.2 %shard_map.37 = (f32[1,16,128]{2,1,0:T(8,128)S(1)}, f32[2,2,256,256]{3,2,1,0:T(8,128)S(1)}) custom-call(f32[1,16,128]{2,1,0:T(8,128)} %bitcast.14, bf16[2,2,256,256]{3,2,1,0:T(8,128)(2,1)} %constant.28.clone.table_ref), custom_call_target="tpu_custom_call" | custom-call | flops 1000000000 | bytes 1000000 | tf_op jit(solution)/shard_map/pallas_call | solution.py:222
  5.3 0.6 %collective-permute-done = f32[1,16,128]{2,1,0:T(8,128)S(1)} collective-permute-done((f32[1,16,128]{2,1,0:T(8,128)}, f32[1,16,128]{2,1,0:T(8,128)S(1)}, u32[]{:S(2)}, u32[]{:S(2)}) %collective-permute-start) | collective-permute-done | bytes 8224 | tf_op jit(solution)/shard_map/ppermute | solution.py:265
  5.9 1.9 %collective-permute-start.1 = (f32[2,16,128]{2,1,0:T(8,128)S(1)}, f32[2,16,128]{2,1,0:T(8,128)S(1)}, u32[]{:S(2)}, u32[]{:S(2)}) collective-permute-start(f32[2,16,128]{2,1,0:T(8,128)S(1)} %pad_maximum_fusion.4), channel_id=1, source_target_pairs={{0,1},{1,0},{2,3},{3,2},{4,5},{5,4},{6,7},{7,6},{8,9},{9,8},{10,11... | collective-permute-start | bytes 49160 | tf_op jit(solution)/shard_map/ppermute | solution.py:265
  7.8 1.7 %shard_map.38.weight_ref = f32[2,192,512]{2,1,0:T(8,128)S(1)} custom-call(s32[2]{0:T(128)S(1)} %pad_add_fusion.offset_ref, bf16[2,2,256,512]{3,2,1,0:T(8,128)(2,1)} %constant.27.clone.table_ref), custom_call_target="tpu_custom_call" | custom-call | flops 1000000000 | bytes 1000000 | tf_op jit(solution)/shard_map/pallas_call | solution.py:222
  9.5 0.2 collective-permute-done.1
  9.7 1.8 %collective-permute-start.2 = (f32[4,16,128]{2,1,0:T(8,128)S(1)}, f32[4,16,128]{2,1,0:T(8,128)S(1)}, u32[]{:S(2)}, u32[]{:S(2)}) collective-permute-start(f32[4,16,128]{2,1,0:T(8,128)S(1)} %pad_maximum_fusion.3), channel_id=1, source_target_pairs={{0,8},{1,9},{2,10},{3,11},{4,12},{5,13},{6,14},{7,15},{8,0},{9,1},... | collective-permute-start | bytes 98312 | tf_op jit(solution)/shard_map/ppermute | solution.py:265
  11.5 2.1 %collective-permute-done.2 = f32[4,16,128]{2,1,0:T(8,128)S(1)} collective-permute-done((f32[4,16,128]{2,1,0:T(8,128)S(1)}, f32[4,16,128]{2,1,0:T(8,128)S(1)}, u32[]{:S(2)}, u32[]{:S(2)}) %collective-permute-start.2) | collective-permute-done | bytes 32800 | tf_op jit(solution)/shard_map/ppermute | solution.py:265
  13.6 1.9 %collective-permute-start.3 = (f32[8,16,128]{2,1,0:T(8,128)S(1)}, f32[8,16,128]{2,1,0:T(8,128)S(1)}, u32[]{:S(2)}, u32[]{:S(2)}) collective-permute-start(f32[8,16,128]{2,1,0:T(8,128)S(1)} %pad_maximum_fusion.2), channel_id=1, source_target_pairs={{0,16},{1,17},{2,18},{3,19},{4,20},{5,21},{6,22},{7,23},{8,24},{9,... | collective-permute-start | bytes 196616 | tf_op jit(solution)/shard_map/ppermute | solution.py:265
  15.4 2.4 %collective-permute-done.3 = f32[8,16,128]{2,1,0:T(8,128)S(1)} collective-permute-done((f32[8,16,128]{2,1,0:T(8,128)S(1)}, f32[8,16,128]{2,1,0:T(8,128)S(1)}, u32[]{:S(2)}, u32[]{:S(2)}) %collective-permute-start.3) | collective-permute-done | bytes 65568 | tf_op jit(solution)/shard_map/ppermute | solution.py:265
  17.9 0.1 collective-permute-start.4
  17.9 1.3 %collective-permute-done.4 = f32[16,16,128]{2,1,0:T(8,128)S(1)} collective-permute-done((f32[16,16,128]{2,1,0:T(8,128)S(1)}, f32[16,16,128]{2,1,0:T(8,128)S(1)}, u32[]{:S(2)}, u32[]{:S(2)}) %collective-permute-start.4) | collective-permute-done | bytes 131104 | tf_op jit(solution)/shard_map/ppermute | solution.py:265
  19.3 5.5 %shard_map.39 = f32[16384,128]{1,0:T(8,128)} custom-call(s32[1]{0:T(128)} %bitcast.key_ref, f32[32,16,128]{2,1,0:T(8,128)S(1)} %pad_maximum_fusion.rec_ref, f32[2,192,512]{2,1,0:T(8,128)S(1)} %shard_map.38.weight_ref, f32[2,2,256,256]{3,2,1,0:T(8,128)S(1)} %get-tuple-element.16.dft_ref), custom_call_target="tpu_custom_call" | custom-call | flops 10000000000 | bytes 10000000 | tf_op jit(solution)/shard_map/pallas_call | solution.py:278
  (5 shorter events, 0.0 us)
Async XLA Ops:
  0.0 5.9 %collective-permute-start = (f32[1,16,128]{2,1,0:T(8,128)}, f32[1,16,128]{2,1,0:T(8,128)S(1)}, u32[]{:S(2)}, u32[]{:S(2)}) collective-permute-start(f32[1,16,128]{2,1,0:T(8,128)} %bitcast.13), channel_id=1, source_target_pairs={{0,2},{1,3},{2,0},{3,1},{4,6},{5,7},{6,4},{7,5},{8,10},{9,11},{10,... | collective-permute-start | bytes 24584 | tf_op jit(solution)/shard_map/ppermute | solution.py:265
  5.9 3.7 %collective-permute-start.1 = (f32[2,16,128]{2,1,0:T(8,128)S(1)}, f32[2,16,128]{2,1,0:T(8,128)S(1)}, u32[]{:S(2)}, u32[]{:S(2)}) collective-permute-start(f32[2,16,128]{2,1,0:T(8,128)S(1)} %pad_maximum_fusion.4), channel_id=1, source_target_pairs={{0,1},{1,0},{2,3},{3,2},{4,5},{5,4},{6,7},{7,6},{8,9},{9,8},{10,11... | collective-permute-start | bytes 49160 | tf_op jit(solution)/shard_map/ppermute | solution.py:265
  9.7 3.9 %collective-permute-start.2 = (f32[4,16,128]{2,1,0:T(8,128)S(1)}, f32[4,16,128]{2,1,0:T(8,128)S(1)}, u32[]{:S(2)}, u32[]{:S(2)}) collective-permute-start(f32[4,16,128]{2,1,0:T(8,128)S(1)} %pad_maximum_fusion.3), channel_id=1, source_target_pairs={{0,8},{1,9},{2,10},{3,11},{4,12},{5,13},{6,14},{7,15},{8,0},{9,1},... | collective-permute-start | bytes 98312 | tf_op jit(solution)/shard_map/ppermute | solution.py:265
  13.6 4.3 %collective-permute-start.3 = (f32[8,16,128]{2,1,0:T(8,128)S(1)}, f32[8,16,128]{2,1,0:T(8,128)S(1)}, u32[]{:S(2)}, u32[]{:S(2)}) collective-permute-start(f32[8,16,128]{2,1,0:T(8,128)S(1)} %pad_maximum_fusion.2), channel_id=1, source_target_pairs={{0,16},{1,17},{2,18},{3,19},{4,20},{5,21},{6,22},{7,23},{8,24},{9,... | collective-permute-start | bytes 196616 | tf_op jit(solution)/shard_map/ppermute | solution.py:265
  17.9 1.4 %collective-permute-start.4 = (f32[16,16,128]{2,1,0:T(8,128)S(1)}, f32[16,16,128]{2,1,0:T(8,128)S(1)}, u32[]{:S(2)}, u32[]{:S(2)}) collective-permute-start(f32[16,16,128]{2,1,0:T(8,128)S(1)} %pad_maximum_fusion.1), channel_id=1, source_target_pairs={{0,4},{1,5},{2,6},{3,7},{4,0},{5,1},{6,2},{7,3},{8,12},{9,13},{10,... | collective-permute-start | bytes 393224 | tf_op jit(solution)/shard_map/ppermute | solution.py:265
